TPU v7x, 1024 devices: a whole 4x4x32 slice. The times are simulated.
1024 devices in a mesh: dp: 32 (over x, z_lo), fsdp: 8 (over z_hi, core), tp: 4 (over y).
Axes of the slice: x: 4, y: 4, z: 32 (z_hi: 4, z_lo: 8; z = z_hi * 8 + z_lo), core: 2. Of those that a mesh axis runs over, the one named last changes fastest.
Arguments:
- hidden: bfloat16 [131072, 7168], P(('dp', 'fsdp')), may hold values from -6 to 6
- cotangent: bfloat16 [131072, 576], P(('dp', 'fsdp'), 'tp'), may hold values from -6 to 6
- rewards: int32 [1024], P(('dp', 'fsdp')), may hold values from 0 to 8
- groups: int32 [1024], P(('dp', 'fsdp')), may hold values from 0 to 63, as said below
- lengths: int32 [1024], P(('dp', 'fsdp')), may hold values from 1 to 128
- master: float32 [8, 896, 576], P('fsdp', 'dp', 'tp'), may hold values from -6 to 6
Outputs:
- grad_owned: float32 [8, 896, 576], P('fsdp', 'dp', 'tp')
- rollout: bfloat16 [8, 896, 576], P('fsdp')
Inputs may be any that keep to these rules, and one draw needn't show every extreme that they name: `groups`: each prompt number names exactly 16 samples.
All inputs are finite; a program needn't handle non-finite values.
Results may differ from a plain program's by a relative error of at most 0.0033.
Values may be sent and summed in bfloat16 or wider, within the bound.
No kernel may reach another device: no remote copies, remote signals or barrier semaphores. Data moves between devices by JAX's collectives and lax.ppermute only.
A program may use at most 64 MiB of HBM per device.

v0:
```python
import jax
import jax.numpy as jnp
from jax import lax
from jax.sharding import Mesh
from jax.sharding import PartitionSpec as P

D = 7168
GROUP = 16
FSDP = ("fsdp_0", "fsdp_1")
DP = ("dp_0", "dp_1")
DP_FSDP = ("dp_0", "dp_1", "fsdp_0", "fsdp_1")


def over_axes(array, axes):
    for axis in axes:
        array = lax.psum(array, axis)
    return array


def split_up(array, dim, devices):
    dims = array.shape
    pieces = array.reshape(*dims[:dim], devices, dims[dim] // devices, *dims[dim + 1 :])
    return jnp.moveaxis(pieces, dim, 0)


def sum_at_owner(array, axis, dim):
    pieces = split_up(array, dim, lax.axis_size(axis))
    arrived = lax.all_to_all(pieces, axis, split_axis=0, concat_axis=0, tiled=True)
    return arrived.sum(axis=0)


def copy_for_each(array, axis):
    copies = jnp.broadcast_to(array, (lax.axis_size(axis), *array.shape))
    return lax.all_to_all(copies, axis, split_axis=0, concat_axis=0, tiled=True)


def in_order(pieces, dim):
    pieces = jnp.moveaxis(pieces, 0, dim)
    dims = pieces.shape
    return pieces.reshape(*dims[:dim], dims[dim] * dims[dim + 1], *dims[dim + 2 :])


def gathered_copies(array, axis, dim):
    pieces = copy_for_each(array, axis)
    return in_order(pieces, dim)


def exact_dot(left, right):
    return jnp.dot(left, right, precision=lax.Precision.HIGHEST)


def shards(hidden, cotangent, rewards, groups, lengths, master):
    fsdp_size = lax.axis_size(FSDP)
    dp_size = lax.axis_size(DP)
    samp_local = rewards.shape[0]
    group_count = samp_local * dp_size * fsdp_size // GROUP
    labels = jnp.arange(group_count, dtype=jnp.int32)
    reward_f = rewards.astype(jnp.float32)
    local_onehot = (groups[:, None] == labels[None, :]).astype(jnp.float32)
    totals, squares = (
        over_axes(exact_dot(reward_f, local_onehot), DP_FSDP),
        over_axes(exact_dot(reward_f * reward_f, local_onehot), DP_FSDP),
    )
    group_mean = totals / GROUP
    group_square = squares / GROUP
    sample_mean = exact_dot(local_onehot, group_mean)
    sample_square = exact_dot(local_onehot, group_square)
    advantage = (reward_f - sample_mean) / jnp.sqrt(sample_square - sample_mean * sample_mean + 1.0)
    seq_len = hidden.shape[0] // samp_local
    positions = jnp.arange(seq_len, dtype=jnp.int32)
    live = (positions[None, :] < lengths[:, None]).astype(jnp.float32)
    scale = (advantage[:, None] * live / lengths[:, None].astype(jnp.float32)).reshape(
        hidden.shape[0]
    )
    weighted = (cotangent.astype(jnp.float32) * scale[:, None]).astype(jnp.bfloat16)
    cols_local = cotangent.shape[1]
    block_rows = D // fsdp_size
    product = jnp.einsum("td,tc->dc", hidden, weighted, preferred_element_type=jnp.float32)
    reduced = lax.psum_scatter(
        product.reshape(1 * lax.axis_size(FSDP), block_rows, cols_local),
        FSDP,
        scatter_dimension=0,
        tiled=True,
    )
    owned = sum_at_owner(reduced, DP, 1)
    updated = (master - 0.1 * owned).astype(jnp.bfloat16)
    row_block = gathered_copies(updated, DP, 1)
    rollout = gathered_copies(row_block, "tp", 2)
    return (owned, rollout)


def solution(mesh):
    torus = Mesh(
        mesh.devices.reshape(4, 8, 4, 2, mesh.shape["tp"]),
        ("dp_0", "dp_1", "fsdp_0", "fsdp_1", "tp"),
    )
    placed = (
        P(DP_FSDP, None),
        P(DP_FSDP, "tp"),
        P(DP_FSDP),
        P(DP_FSDP),
        P(DP_FSDP),
        P(FSDP, DP, "tp"),
    )
    return jax.shard_map(
        shards,
        mesh=torus,
        in_specs=placed,
        out_specs=(P(FSDP, DP, "tp"), P(FSDP, None, None)),
        check_vma=False,
    )
```

profile of v0, /device:TPU:1, one launch (start us, length us, event | category | flops | bytes accessed | tf_op | source)
XLA Modules:
  0.0 395.8 jit_solution(7621795865842253681)
XLA Ops:
  7.2 0.0 reduce-scatter.2.cloned.1.call-start
  7.2 0.9 convolution_bitcast_fusion.1
  8.1 0.9 convolution_bitcast_fusion.3
  8.9 0.7 convert_element_type.22
  9.6 9.3 %all-reduce.2 = (f32[64]{0:T(128)S(1)}, f32[64]{0:T(128)S(1)}) all-reduce(f32[64]{0:T(128)S(1)} %convolution_bitcast_fusion.3, f32[64]{0:T(128)S(1)} %convolution_bitcast_fusion.1), channel_id=1, replica_groups=mesh['dp_0'=4,'dp_1'=8,'fsdp_0'=4,'fsdp_1'=2,'tp'=4] {'dp_0'}, use_global_device_ids=true, to_apply=%region_0.0 | all-reduce | flops 128 | bytes 1024 | tf_op jit(solution)/shard_map/psum | solution.py:16
  18.9 32.5 %all-reduce = (f32[64]{0:T(128)S(1)}, f32[64]{0:T(128)S(1)}) all-reduce(f32[64]{0:T(128)S(1)} %get-tuple-element.6, f32[64]{0:T(128)S(1)} %get-tuple-element.7), channel_id=1, replica_groups=mesh['dp_0'=4,'dp_1'=8,'fsdp_0'=4,'fsdp_1'=2,'tp'=4] {'dp_1'}, use_global_device_ids=true, to_apply=%region_1.0 | all-reduce | flops 128 | bytes 1024 | tf_op jit(solution)/shard_map/psum | solution.py:16
  51.3 27.0 %all-reduce.1 = (f32[64]{0:T(128)S(1)}, f32[64]{0:T(128)S(1)}) all-reduce(f32[64]{0:T(128)S(1)} %get-tuple-element.2, f32[64]{0:T(128)S(1)} %get-tuple-element.3), channel_id=1, replica_groups=mesh['dp_0'=4,'dp_1'=8,'fsdp_0'=4,'fsdp_1'=2,'tp'=4] {'fsdp_0'}, use_global_device_ids=true, to_apply=%region_2.0 | all-reduce | flops 128 | bytes 1024 | tf_op jit(solution)/shard_map/psum | solution.py:16
  78.4 10.6 %all-reduce.3 = (f32[64]{0:T(128)S(1)}, f32[64]{0:T(128)S(1)}) all-reduce(f32[64]{0:T(128)S(1)} %get-tuple-element.4, f32[64]{0:T(128)S(1)} %get-tuple-element.5), channel_id=1, replica_groups=mesh['dp_0'=4,'dp_1'=8,'fsdp_0'=4,'fsdp_1'=2,'tp'=4] {'fsdp_1'}, use_global_device_ids=true, to_apply=%region_3.0 | all-reduce | flops 128 | bytes 1024 | tf_op jit(solution)/shard_map/psum | solution.py:16
  88.9 0.8 convolution_bitcast_fusion.2
  89.8 0.9 fusion.3
  90.7 0.7 divide_bitcast_fusion
  91.4 4.4 %fusion.4 = f32[144,7168]{1,0:T(8,128)S(1)} fusion(bf16[512,7168]{1,0:T(8,128)(2,1)} %param.6, bf16[512,144]{0,1:T(8,128)(2,1)} %param.7, f32[512]{0:T(512)S(1)} %divide_bitcast_fusion), kind=kOutput, calls=%fused_computation.10 | convolution fusion | flops 1057185792 | bytes 11618304 | tf_op jit(solution)/shard_map/td,tc->dc/dot_general | solution.py:78
  95.8 0.0 copy-start
  95.8 2.2 copy.18
  98.0 0.0 reduce-scatter.2.cloned.1.call-update
  98.0 194.0 %reduce-scatter.2.cloned.1.call-done = f32[1,896,144]{1,2,0:T(8,128)} async-done(((f32[8,896,144]{1,2,0:T(8,128)}), f32[1,896,144]{1,2,0:T(8,128)}) %reduce-scatter.2.cloned.1.call-update) | async-done | bytes 516112 | tf_op jit(solution)/shard_map/reduce_scatter | solution.py:79
  292.0 2.5 copy.12
  294.6 48.3 %all_to_all.15 = f32[32,1,28,144]{3,1,2,0:T(1,128)S(1)} all-to-all(f32[32,1,28,144]{3,1,2,0:T(1,128)S(1)} %bitcast.46), channel_id=1, replica_groups=mesh['dp_0'=4,'dp_1'=8,'fsdp_0'=4,'fsdp_1'=2,'tp'=4] {'dp_0','dp_1'}, dimensions={0} | all-to-all | bytes 1032192 | tf_op jit(solution)/shard_map/all_to_all | solution.py:28
  342.8 0.6 reduce_sum.11
  343.5 0.0 copy-done
  343.5 0.1 broadcast_in_dim.4
  343.6 0.7 reshape.68
  344.3 24.6 %all_to_all.16 = bf16[32,2,2016]{2,1,0:T(2,128)(2,1)S(1)} all-to-all(bf16[32,2,2016]{2,1,0:T(2,128)(2,1)S(1)} %reshape.68), channel_id=1, replica_groups=mesh['dp_0'=4,'dp_1'=8,'fsdp_0'=4,'fsdp_1'=2,'tp'=4] {'dp_0','dp_1'}, dimensions={0} | all-to-all | bytes 516096 | tf_op jit(solution)/shard_map/all_to_all | solution.py:34
  368.9 0.7 reshape.69
  369.6 0.2 reshape_transpose.3
  369.8 0.2 copy.13
  370.0 1.0 broadcast_in_dim.5
  371.0 3.6 all-to-all-start.2
  374.6 0.6 reduce_sum.12
  375.3 12.7 %all-to-all-done.2 = bf16[4,1,896,144]{2,3,1,0:T(8,128)(2,1)S(1)} async-done(((bf16[4,1,896,144]{2,3,1,0:T(8,128)(2,1)}), bf16[4,1,896,144]{2,3,1,0:T(8,128)(2,1)S(1)}, u32[]{:S(2)}, u32[]{:S(2)}) %all-to-all-start.2) | async-done | bytes 1032224 | tf_op jit(solution)/shard_map/all_to_all | solution.py:34
  388.0 1.0 copy.21
  (2 shorter events, 0.1 us)
Async XLA Ops:
  7.2 284.8 %reduce-scatter.2.cloned.1.call-start = ((), (), s32[]{:S(2)}) async-start(), calls=%async_computation.4 | async-start | bytes 4644864 | tf_op jit(solution)/shard_map/reduce_scatter | solution.py:79
  95.8 247.6 %copy-start = (f32[1,28,144]{2,0,1:T(1,128)S(1)}, f32[1,28,144]{2,0,1:T(1,128)}, u32[]{:S(2)}) copy-start(f32[1,28,144]{2,0,1:T(1,128)} %param.11) | copy-start | bytes 48388
  371.0 16.9 %all-to-all-start.2 = ((bf16[4,1,896,144]{2,3,1,0:T(8,128)(2,1)}), bf16[4,1,896,144]{2,3,1,0:T(8,128)(2,1)S(1)}, u32[]{:S(2)}, u32[]{:S(2)}) async-start(bf16[4,1,896,144]{2,3,1,0:T(8,128)(2,1)} %broadcast_in_dim.5), calls=%async_computation.3 | async-start | bytes 2064384 | tf_op jit(solution)/shard_map/all_to_all | solution.py:34
Sparse Core Ops, SparseCore 0:
  98.2 193.7 reduce-scatter.1
where the time goes:
time: 396 us
  waiting for transfers between devices  207 us (52%)
  blocking collectives  152 us (38%)
  between operations  14.1 us (4%)
  local copies, waits for them, and re-layouts  9.19 us (2%)
  matrix products  7.84 us (2%)
    reduce_scatter x1, waiting for transfers between devices, shards(): lax.psum_scatter(product.reshape(1 * lax.axis_size(FSDP), block_rows, col...  194 us
    psum x4, blocking collectives, over_axes(): array = lax.psum(array, axis)  79.3 us
    all_to_all x1, blocking collectives, sum_at_owner(): lax.all_to_all(pieces, axis, split_axis=0, concat_axis=0, tiled=True)  48.3 us
    all_to_all x1, blocking collectives, copy_for_each(): return lax.all_to_all(copies, axis, split_axis=0, concat_axis=0, tiled=True)  24.6 us
    all_to_all x1, waiting for transfers between devices, copy_for_each(): return lax.all_to_all(copies, axis, split_axis=0, concat_axis=0, tiled=True)  12.7 us
  transfers between devices with their start and end apart: 2, of which 2 were waited for; matrix products, arithmetic and copies ran while one was open for 0% of the time, Pallas kernels for 0%

commit v1 on v0

v1 whole, which is shorter than its diff:
```python
import jax
import jax.numpy as jnp
from jax import lax
from jax.experimental import pallas as pl
from jax.experimental.pallas import tpu as pltpu
from jax.sharding import Mesh
from jax.sharding import PartitionSpec as P

GROUP = 16
X, ZL, ZH, CORE, TP = "x", "z_lo", "z_hi", "core", "tp"
DP = (X, ZL)
FSDP = (ZH, CORE)
DP_FSDP = (X, ZL, ZH, CORE)

ROWS = 896
COLS = 144
OWN = 28
QROW = 40
LANE = 128
f32 = jnp.float32
bf16 = jnp.bfloat16


def lane_iota(rows):
    return lax.broadcasted_iota(jnp.int32, (rows, LANE), 1)


def roll(tile, shift):
    shift = shift % LANE
    return tile if shift == 0 else pltpu.roll(tile, shift, 1)


def put(acc, tiles, src, dst, width):
    lane = lane_iota(acc.shape[0])
    done = 0
    while done < width:
        tile, off = divmod(src + done, LANE)
        take = min(LANE - off, width - done)
        at = dst + done
        moved = roll(tiles(tile), at - off)
        acc = jnp.where((lane >= at) & (lane < at + take), moved, acc)
        done += take
    return acc


def grad_body(scal, seen, own_c, oth_c, own_h, oth_h, out, w_own, w_oth, prod):
    step = pl.program_id(0)

    @pl.when(step == 0)
    def _():
        seen_r = seen[:, 0:32].astype(f32)
        seen_g = seen[:, 32:64]
        pos = lax.broadcasted_iota(jnp.int32, (1, LANE), 1)
        for s in range(8):
            hit = seen_g == scal[9 + s]
            total = jnp.sum(jnp.where(hit, seen_r, 0.0), axis=(0, 1), keepdims=True)
            square = jnp.sum(jnp.where(hit, seen_r * seen_r, 0.0), axis=(0, 1), keepdims=True)
            mean = total / GROUP
            var = square / GROUP - mean * mean
            reward = jnp.full((1, 1), scal[1 + s], jnp.int32).astype(f32)
            adv = (reward - mean) / jnp.sqrt(var + 1.0)
            size = jnp.full((1, 1), scal[17 + s], jnp.int32).astype(f32)
            live = jnp.where(pos < scal[17 + s], 1.0, 0.0)
            scale = adv * live / size
            src, dst = (own_c, w_own) if s < 4 else (oth_c, w_oth)
            at = (s % 4) * LANE
            dst[:, at : at + LANE] = (src[:, at : at + LANE].astype(f32) * scale).astype(bf16)

    block = jnp.dot(w_own[...], own_h[...], preferred_element_type=f32)
    block += jnp.dot(w_oth[...], oth_h[...], preferred_element_type=f32)
    prod[step] = block

    @pl.when(step == pl.num_programs(0) - 1)
    def _():
        for x in range(4):
            for t in range(ROWS // LANE):
                acc = jnp.zeros((COLS, LANE), f32)
                for j in range(4):
                    lo = max(j * 224, t * LANE)
                    hi = min(j * 224 + 224, t * LANE + LANE)
                    if lo < hi:
                        at = x * 224 + lo - j * 224
                        tiles = lambda k, j=j: prod[j, :, k * LANE : (k + 1) * LANE]
                        acc = put(acc, tiles, at, lo - t * LANE, hi - lo)
                out[x, :, t * LANE : (t + 1) * LANE] = acc.astype(bf16)


def grad_parts(scal, seen, own_c, oth_c, own_h, oth_h):
    tokens = own_h.shape[0]
    half = pl.BlockSpec((tokens, ROWS), lambda j, scal: (0, 2 * j + scal[0]))
    whole = lambda shape: pl.BlockSpec(shape, lambda j, scal: (0,) * len(shape))
    return pl.pallas_call(
        grad_body,
        out_shape=jax.ShapeDtypeStruct((4, COLS, ROWS), bf16),
        grid_spec=pltpu.PrefetchScalarGridSpec(
            num_scalar_prefetch=1,
            grid=(4,),
            in_specs=[
                whole(seen.shape),
                whole(own_c.shape),
                whole(oth_c.shape),
                half,
                half,
            ],
            out_specs=whole((4, COLS, ROWS)),
            scratch_shapes=[
                pltpu.VMEM((COLS, tokens), bf16),
                pltpu.VMEM((COLS, tokens), bf16),
                pltpu.VMEM((4, COLS, ROWS), f32),
            ],
        ),
        compiler_params=pltpu.CompilerParams(dimension_semantics=("arbitrary",)),
        name="grad_parts",
    )(scal, seen, own_c, oth_c, own_h, oth_h)


def x_body(parts, out, total):
    for t in range(ROWS // LANE):
        at = slice(t * LANE, (t + 1) * LANE)
        total[t] = (parts[0, :, at].astype(f32) + parts[1, :, at].astype(f32)) + (
            parts[2, :, at].astype(f32) + parts[3, :, at].astype(f32)
        )
    for z in range(8):
        acc = jnp.zeros((COLS, LANE), f32)
        for j in range(4):
            acc = put(acc, lambda k: total[k], j * 224 + z * OWN, j * 32, OWN)
        out[z] = acc.astype(bf16)


def x_sum(parts):
    return pl.pallas_call(
        x_body,
        out_shape=jax.ShapeDtypeStruct((8, COLS, LANE), bf16),
        scratch_shapes=[pltpu.VMEM((ROWS // LANE, COLS, LANE), f32)],
        name="x_sum",
    )(parts)


def zl_body(parts, out, total):
    acc = parts[0].astype(f32)
    for z in range(1, 8):
        acc += parts[z].astype(f32)
    total[0:COLS] = acc
    total[COLS:] = jnp.zeros((4 * QROW - COLS, LANE), f32)
    for j in range(4):
        acc = jnp.zeros((QROW, LANE), f32)
        for q in range(4):
            rows = total[q * QROW : (q + 1) * QROW]
            acc = put(acc, lambda k: rows, j * 32, q * 32, 32)
        out[j] = acc.astype(bf16)


def zl_sum(parts):
    return pl.pallas_call(
        zl_body,
        out_shape=jax.ShapeDtypeStruct((4, QROW, LANE), bf16),
        scratch_shapes=[pltpu.VMEM((4 * QROW, LANE), f32)],
        name="zl_sum",
    )(parts)


def zh_body(parts, master, grad, copies):
    total = (parts[0].astype(f32) + parts[1].astype(f32)) + (
        parts[2].astype(f32) + parts[3].astype(f32)
    )
    grad[...] = total
    new = (master[...] - 0.1 * total).astype(bf16)
    for z in range(8):
        copies[z] = new


def zh_sum(parts, master):
    return pl.pallas_call(
        zh_body,
        out_shape=(
            jax.ShapeDtypeStruct((QROW, LANE), f32),
            jax.ShapeDtypeStruct((8, QROW, LANE), bf16),
        ),
        name="zh_sum",
    )(parts, master)


def rows_body(parts, out, wide):
    for x in range(4):
        for z in range(8):
            wide[x * 8 + z] = parts[x, z].astype(f32)
    for t in range(ROWS // LANE):
        for q in range(4):
            acc = jnp.zeros((QROW, LANE), f32)
            for d in range(32):
                lo = max(d * OWN, t * LANE)
                hi = min(d * OWN + OWN, t * LANE + LANE)
                if lo < hi:
                    acc = put(acc, lambda k: wide[d], q * 32 + lo - d * OWN, lo - t * LANE, hi - lo)
            rows = min(QROW, COLS - q * QROW)
            out[q * QROW : q * QROW + rows, t * LANE : (t + 1) * LANE] = acc[:rows].astype(bf16)


def row_block(parts):
    return pl.pallas_call(
        rows_body,
        out_shape=jax.ShapeDtypeStruct((COLS, ROWS), bf16),
        scratch_shapes=[pltpu.VMEM((32, QROW, LANE), f32)],
        name="row_block",
    )(parts)


def pack(master):
    wide = jnp.pad(master.T, ((0, 4 * QROW - COLS), (0, 32 - OWN)))
    return wide.reshape(4, QROW, 32).transpose(1, 0, 2).reshape(QROW, LANE)


def unpack(grad):
    wide = grad.reshape(QROW, 4, 32).transpose(1, 0, 2).reshape(4 * QROW, 32)
    return wide[:COLS, :OWN].T


def exchange(array, axis):
    return lax.all_to_all(array, axis, split_axis=0, concat_axis=0, tiled=True)


def shards(hidden, cotangent, rewards, groups, lengths, master):
    swap = [(0, 1), (1, 0)]
    other_hidden = lax.ppermute(hidden, CORE, swap)
    cot = cotangent.T
    other_cot = lax.ppermute(cot, CORE, swap)
    mine = jnp.stack([rewards, groups, lengths])
    chip = lax.all_gather(mine, CORE)
    other = chip[0] + chip[1] - mine
    plane = lax.all_gather(chip[:, :2], X)
    line = plane.transpose(2, 0, 1, 3).reshape(64)
    copies = jnp.broadcast_to(jnp.pad(line, (0, 64)), (32, LANE))
    seen = exchange(copies, (ZH, ZL))
    core = lax.axis_index(CORE).astype(jnp.int32)
    scal = jnp.concatenate([core[None], jnp.stack([mine, other], axis=1).reshape(24)])
    parts = grad_parts(scal, seen, cot, other_cot, hidden, other_hidden)
    parts = x_sum(exchange(parts, X))
    parts = zl_sum(exchange(parts, ZL))
    grad, copies = zh_sum(exchange(parts, ZH), pack(master[0]))
    line = exchange(copies, ZL)
    plane = lax.all_gather(line, X)
    block = row_block(plane)
    rollout = lax.all_gather(block, TP)
    rollout = rollout.reshape(4 * COLS, ROWS).T
    return (unpack(grad)[None], rollout[None])


def solution(mesh):
    torus = Mesh(
        mesh.devices.reshape(4, 8, 4, 2, mesh.shape["tp"]),
        (X, ZL, ZH, CORE, TP),
    )
    placed = (
        P(DP_FSDP, None),
        P(DP_FSDP, TP),
        P(DP_FSDP),
        P(DP_FSDP),
        P(DP_FSDP),
        P(FSDP, DP, TP),
    )
    return jax.shard_map(
        shards,
        mesh=torus,
        in_specs=placed,
        out_specs=(P(FSDP, DP, TP), P(FSDP, None, None)),
        check_vma=False,
    )
```

time: 396 us -> 206 us (0.52)
  the two profiles are of different devices: /device:TPU:1 before, /device:TPU:8 now
where the time goes in v1:
time: 206 us; the launch traced here: 205 us
  blocking collectives  84.4 us (41%)
  waiting for transfers between devices  49.8 us (24%)
  starting transfers between devices  47.8 us (23%)
  Pallas kernels  15 us (7%)
  local copies, waits for them, and re-layouts  5.59 us (3%)
  other arithmetic  2.06 us (1%)
    all_to_all x3, waiting for transfers between devices, exchange(): return lax.all_to_all(array, axis, split_axis=0, concat_axis=0, tiled=True)  49.8 us
    all_to_all x3, starting transfers between devices, exchange(): return lax.all_to_all(array, axis, split_axis=0, concat_axis=0, tiled=True)  43.9 us
    all_to_all x2, blocking collectives, exchange(): return lax.all_to_all(array, axis, split_axis=0, concat_axis=0, tiled=True)  34.7 us
    all_gather x1, blocking collectives, shards(): rollout = lax.all_gather(block, TP)  14.2 us
    all_gather x1, blocking collectives, shards(): plane = lax.all_gather(line, X)  13.1 us
    all_gather x1, blocking collectives, shards(): chip = lax.all_gather(mine, CORE)  11.3 us
    all_gather x1, blocking collectives, shards(): plane = lax.all_gather(chip[:, :2], X)  11.2 us
    pallas_call x1, Pallas kernels, grad_parts(): pl.pallas_call(grad_body, out_shape=jax.ShapeDtypeStruct((4, COLS, ROWS),...  7.41 us
  transfers between devices with their start and end apart: 5, of which 3 were waited for; matrix products, arithmetic and copies ran while one was open for 3% of the time, Pallas kernels for 0%

profile of v1, /device:TPU:8, one launch (start us, length us, event | category | flops | bytes accessed | tf_op | source)
XLA Modules:
  0.0 205.5 jit_solution(7923133326026883939)
XLA Ops:
  0.6 1.9 collective-permute-start.1
  2.6 0.7 fusion.3
  3.3 11.3 %all-gather.4 = s32[2,3,4]{2,1,0:T(4,128)S(1)} all-gather(s32[1,3,4]{2,1,0:T(4,128)S(1)} %get-tuple-element.11), channel_id=2, replica_groups=mesh['x'=4,'z_lo'=8,'z_hi'=4,'core'=2,'tp'=4] {'core'}, dimensions={0}, use_global_device_ids=true | all-gather | bytes 144 | tf_op jit(solution)/shard_map/all_gather | solution.py:228
  14.5 11.2 %all-gather.1 = s32[8,2,4]{2,1,0:T(2,128)S(1)} all-gather(s32[2,2,4]{2,1,0:T(2,128)S(1)} %slice.22), channel_id=3, replica_groups=mesh['x'=4,'z_lo'=8,'z_hi'=4,'core'=2,'tp'=4] {'x'}, dimensions={0}, use_global_device_ids=true | all-gather | bytes 320 | tf_op jit(solution)/shard_map/all_gather | solution.py:230
  25.7 0.1 reshape.93
  25.8 0.6 broadcast_in_dim.13
  26.4 28.7 %all-to-all-start = ((s32[32,1,128]{2,1,0:T(1,128)}), s32[32,1,128]{2,1,0:T(1,128)S(1)}, u32[]{:S(2)}, u32[]{:S(2)}) async-start(s32[32,1,128]{2,1,0:T(1,128)} %broadcast_in_dim.13), calls=%async_computation | async-start | bytes 32768 | tf_op jit(solution)/shard_map/all_to_all | solution.py:219
  55.2 1.9 collective-permute-start
  57.1 0.7 fusion.1
  57.9 0.7 pad_add_fusion.2.scal
  58.6 19.0 %all-to-all-done = s32[32,1,128]{2,1,0:T(1,128)S(1)} async-done(((s32[32,1,128]{2,1,0:T(1,128)}), s32[32,1,128]{2,1,0:T(1,128)S(1)}, u32[]{:S(2)}, u32[]{:S(2)}) %all-to-all-start) | async-done | bytes 16416 | tf_op jit(solution)/shard_map/all_to_all | solution.py:219
  77.5 0.6 copy-done.2
  78.2 7.4 %grad_parts.1 = bf16[4,144,896]{2,1,0:T(8,128)(2,1)} custom-call(s32[25]{0:T(128)} %pad_add_fusion.2.scal, s32[32,128]{1,0:T(8,128)} %bitcast.52, bf16[144,512]{1,0:T(8,128)(2,1)} %bitcast.50, bf16[144,512]{1,0:T(8,128)(2,1)} %copy-done.1, bf16[512,7168]{1,0:T(8,128)(2,1)} %own_h.1, bf16[512,7168]{1,0:T(8,128)(2,1)} %collective-permute-done.1.oth_h), custom_call_target="tpu_custom_call" | custom-call | tf_op jit(solution)/shard_map/grad_parts/pallas_call | solution.py:92
  85.6 15.7 %all_to_all.28.parts = bf16[4,144,896]{2,1,0:T(8,128)(2,1)} all-to-all(bf16[4,144,896]{2,1,0:T(8,128)(2,1)} %grad_parts.1), channel_id=1, replica_groups=mesh['x'=4,'z_lo'=8,'z_hi'=4,'core'=2,'tp'=4] {'x'}, dimensions={0} | all-to-all | bytes 2064384 | tf_op jit(solution)/shard_map/all_to_all | solution.py:219
  101.3 2.4 %x_sum.1 = bf16[8,144,128]{2,1,0:T(8,128)(2,1)} custom-call(bf16[4,144,896]{2,1,0:T(8,128)(2,1)} %all_to_all.28.parts), custom_call_target="tpu_custom_call" | custom-call | tf_op jit(solution)/shard_map/x_sum/pallas_call | solution.py:131
  103.6 19.0 %all_to_all.29.parts = bf16[8,144,128]{2,1,0:T(8,128)(2,1)} all-to-all(bf16[8,144,128]{2,1,0:T(8,128)(2,1)} %x_sum.1), channel_id=1, replica_groups=mesh['x'=4,'z_lo'=8,'z_hi'=4,'core'=2,'tp'=4] {'z_lo'}, dimensions={0} | all-to-all | bytes 589824 | tf_op jit(solution)/shard_map/all_to_all | solution.py:219
  122.6 1.7 zl_sum.1
  124.3 10.8 %all-to-all-start.3 = ((bf16[4,40,128]{2,1,0:T(8,128)(2,1)}), bf16[4,40,128]{2,1,0:T(8,128)(2,1)S(1)}, u32[]{:S(2)}, u32[]{:S(2)}) async-start(bf16[4,40,128]{2,1,0:T(8,128)(2,1)} %zl_sum.1), calls=%async_computation.3 | async-start | bytes 81920 | tf_op jit(solution)/shard_map/all_to_all | solution.py:219
  135.2 0.1 copy.38
  135.4 0.7 reshape.95.master
  136.1 21.5 %all-to-all-done.3.parts = bf16[4,40,128]{2,1,0:T(8,128)(2,1)S(1)} async-done(((bf16[4,40,128]{2,1,0:T(8,128)(2,1)}), bf16[4,40,128]{2,1,0:T(8,128)(2,1)S(1)}, u32[]{:S(2)}, u32[]{:S(2)}) %all-to-all-start.3) | async-done | bytes 40992 | tf_op jit(solution)/shard_map/all_to_all | solution.py:219
  157.6 0.6 copy-done
  158.2 1.4 zh_sum.1
  159.6 4.4 %all-to-all-start.4 = ((bf16[8,40,128]{2,1,0:T(8,128)(2,1)}), bf16[8,40,128]{2,1,0:T(8,128)(2,1)S(1)}, u32[]{:S(2)}, u32[]{:S(2)}) async-start(bf16[8,40,128]{2,1,0:T(8,128)(2,1)} %get-tuple-element.5), calls=%async_computation.4 | async-start | bytes 163840 | tf_op jit(solution)/shard_map/all_to_all | solution.py:219
  164.0 0.8 reshape.96
  165.0 0.1 reshape.97
  165.1 0.6 copy.40
  165.7 9.3 %all-to-all-done.4 = bf16[8,40,128]{2,1,0:T(8,128)(2,1)S(1)} async-done(((bf16[8,40,128]{2,1,0:T(8,128)(2,1)}), bf16[8,40,128]{2,1,0:T(8,128)(2,1)S(1)}, u32[]{:S(2)}, u32[]{:S(2)}) %all-to-all-start.4) | async-done | bytes 81952 | tf_op jit(solution)/shard_map/all_to_all | solution.py:219
  175.1 13.1 %all-gather.2 = bf16[32,40,128]{2,1,0:T(8,128)(2,1)} all-gather(bf16[8,40,128]{2,1,0:T(8,128)(2,1)S(1)} %all-to-all-done.4), channel_id=4, replica_groups=mesh['x'=4,'z_lo'=8,'z_hi'=4,'core'=2,'tp'=4] {'x'}, dimensions={0}, use_global_device_ids=true | all-gather | bytes 409600 | tf_op jit(solution)/shard_map/all_gather | solution.py:241
  188.2 2.1 %row_block.1 = bf16[144,896]{1,0:T(8,128)(2,1)} custom-call(bf16[4,8,40,128]{3,2,1,0:T(8,128)(2,1)} %bitcast.46), custom_call_target="tpu_custom_call" | custom-call | tf_op jit(solution)/shard_map/row_block/pallas_call | solution.py:200
  190.3 14.2 %all-gather.3 = bf16[576,896]{1,0:T(8,128)(2,1)S(1)} all-gather(bf16[144,896]{1,0:T(8,128)(2,1)} %row_block.1), channel_id=5, replica_groups=mesh['x'=4,'z_lo'=8,'z_hi'=4,'core'=2,'tp'=4] {'tp'}, dimensions={0}, use_global_device_ids=true | all-gather | bytes 1290240 | tf_op jit(solution)/shard_map/all_gather | solution.py:243
  204.5 1.0 copy.45
  (19 shorter events, 0.4 us)
Async XLA Ops:
  0.6 76.9 %collective-permute-start.1 = (bf16[512,7168]{1,0:T(8,128)(2,1)}, bf16[512,7168]{1,0:T(8,128)(2,1)}, u32[]{:S(2)}, u32[]{:S(2)}) collective-permute-start(bf16[512,7168]{1,0:T(8,128)(2,1)} %own_h.1), channel_id=1, source_target_pairs={{0,4},{4,0},{1,5},{5,1},{2,6},{6,2},{3,7},{7,3},{8,12},{12,8},{9,1... | collective-permute-start | bytes 22020104 | tf_op jit(solution)/shard_map/ppermute | solution.py:224
  26.4 51.1 %all-to-all-start = ((s32[32,1,128]{2,1,0:T(1,128)}), s32[32,1,128]{2,1,0:T(1,128)S(1)}, u32[]{:S(2)}, u32[]{:S(2)}) async-start(s32[32,1,128]{2,1,0:T(1,128)} %broadcast_in_dim.13), calls=%async_computation | async-start | bytes 32768 | tf_op jit(solution)/shard_map/all_to_all | solution.py:219
  55.2 22.4 %collective-permute-start = (bf16[144,512]{1,0:T(8,128)(2,1)}, bf16[144,512]{1,0:T(8,128)(2,1)S(1)}, u32[]{:S(2)}, u32[]{:S(2)}) collective-permute-start(bf16[144,512]{1,0:T(8,128)(2,1)} %bitcast.49), channel_id=1, source_target_pairs={{0,4},{4,0},{1,5},{5,1},{2,6},{6,2},{3,7},{7,3},{8,12},{12,8},{9,1... | collective-permute-start | bytes 442376 | tf_op jit(solution)/shard_map/ppermute | solution.py:226
  77.5 0.6 copy-start.2
  77.5 0.7 copy-start.1
  78.2 56.9 %copy-start.3 = (f32[1,28,144]{2,0,1:T(1,128)S(1)}, f32[1,28,144]{2,0,1:T(1,128)}, u32[]{:S(2)}) copy-start(f32[1,28,144]{2,0,1:T(1,128)} %param.11) | copy-start | bytes 48388
  124.3 33.2 %all-to-all-start.3 = ((bf16[4,40,128]{2,1,0:T(8,128)(2,1)}), bf16[4,40,128]{2,1,0:T(8,128)(2,1)S(1)}, u32[]{:S(2)}, u32[]{:S(2)}) async-start(bf16[4,40,128]{2,1,0:T(8,128)(2,1)} %zl_sum.1), calls=%async_computation.3 | async-start | bytes 81920 | tf_op jit(solution)/shard_map/all_to_all | solution.py:219
  157.5 0.6 copy-start
  159.6 15.5 %all-to-all-start.4 = ((bf16[8,40,128]{2,1,0:T(8,128)(2,1)}), bf16[8,40,128]{2,1,0:T(8,128)(2,1)S(1)}, u32[]{:S(2)}, u32[]{:S(2)}) async-start(bf16[8,40,128]{2,1,0:T(8,128)(2,1)} %get-tuple-element.5), calls=%async_computation.4 | async-start | bytes 163840 | tf_op jit(solution)/shard_map/all_to_all | solution.py:219

commit v2 on v1

v2 whole, which is shorter than its diff:
```python
import jax
import jax.numpy as jnp
from jax import lax
from jax.experimental import pallas as pl
from jax.experimental.pallas import tpu as pltpu
from jax.sharding import Mesh
from jax.sharding import PartitionSpec as P


GROUP = 16
X, ZL, ZH, CORE, TP = "x", "z_lo", "z_hi", "core", "tp"
DP = (X, ZL)
FSDP = (ZH, CORE)
DP_FSDP = (X, ZL, ZH, CORE)

ROWS = 896
COLS = 144
OWN = 28
PART = 224
STRIPE = 32
REST = 16
LANE = 128
IN_VMEM = pl.BlockSpec(memory_space=pltpu.VMEM)
f32 = jnp.float32
bf16 = jnp.bfloat16


def lane_iota(rows):
    return lax.broadcasted_iota(jnp.int32, (rows, LANE), 1)


def roll(tile, shift):
    shift = shift % LANE
    return tile if shift == 0 else pltpu.roll(tile, shift, 1)


def put(acc, tiles, src, dst, width):
    lane = lane_iota(acc.shape[0])
    done = 0
    while done < width:
        tile, off = divmod(src + done, LANE)
        take = min(LANE - off, width - done)
        at = dst + done
        moved = roll(tiles(tile), at - off)
        acc = jnp.where((lane >= at) & (lane < at + take), moved, acc)
        done += take
    return acc


def grad_body(scal, seen, own_c, oth_c, own_h, oth_h, out, w_own, w_oth, edge):
    step = pl.program_id(0)

    @pl.when(step == 0)
    def _():
        seen_r = seen[:, 0:32].astype(f32)
        seen_g = seen[:, 32:64]
        pos = lax.broadcasted_iota(jnp.int32, (1, LANE), 1)
        for s in range(8):
            hit = seen_g == scal[9 + s]
            total = jnp.sum(jnp.where(hit, seen_r, 0.0), axis=(0, 1), keepdims=True)
            square = jnp.sum(jnp.where(hit, seen_r * seen_r, 0.0), axis=(0, 1), keepdims=True)
            mean = total / GROUP
            var = square / GROUP - mean * mean
            reward = jnp.full((1, 1), scal[1 + s], jnp.int32).astype(f32)
            adv = (reward - mean) / jnp.sqrt(var + 1.0)
            size = jnp.full((1, 1), scal[17 + s], jnp.int32).astype(f32)
            live = jnp.where(pos < scal[17 + s], 1.0, 0.0)
            scale = adv * live / size
            src, dst = (own_c, w_own) if s < 4 else (oth_c, w_oth)
            at = (s % 4) * LANE
            dst[:, at : at + LANE] = (src[:, at : at + LANE].astype(f32) * scale).astype(bf16)

    block = jnp.dot(w_own[...], own_h[...], preferred_element_type=f32)
    block += jnp.dot(w_oth[...], oth_h[...], preferred_element_type=f32)

    def place(j):
        lo, hi = j * PART, (j + 1) * PART
        tiles = lambda k: block[:, k * LANE : (k + 1) * LANE]
        for x in range(4):
            for t in range(lo // LANE, -(-hi // LANE)):
                begin, end = max(lo, t * LANE), min(hi, (t + 1) * LANE)
                acc = edge[x] if t * LANE < lo else jnp.zeros((COLS, LANE), f32)
                acc = put(acc, tiles, x * PART + begin - lo, begin - t * LANE, end - begin)
                if end == (t + 1) * LANE:
                    out[x, :, t * LANE : end] = acc.astype(bf16)
                else:
                    edge[x] = acc

    for j in range(4):
        pl.when(step == j)(lambda j=j: place(j))


def grad_parts(scal, seen, own_c, oth_c, own_h, oth_h):
    tokens = own_h.shape[0]
    half = pl.BlockSpec((tokens, ROWS), lambda j, scal: (0, 2 * j + scal[0]))
    whole = lambda shape: pl.BlockSpec(shape, lambda j, scal: (0,) * len(shape))
    return pl.pallas_call(
        grad_body,
        out_shape=pltpu.VMEM((4, COLS, ROWS), bf16),
        grid_spec=pltpu.PrefetchScalarGridSpec(
            num_scalar_prefetch=1,
            grid=(4,),
            in_specs=[
                IN_VMEM,
                IN_VMEM,
                IN_VMEM,
                half,
                half,
            ],
            out_specs=whole((4, COLS, ROWS)),
            scratch_shapes=[
                pltpu.VMEM((COLS, tokens), bf16),
                pltpu.VMEM((COLS, tokens), bf16),
                pltpu.VMEM((4, COLS, LANE), f32),
            ],
        ),
        compiler_params=pltpu.CompilerParams(dimension_semantics=("arbitrary",)),
        name="grad_parts",
    )(scal, in_vmem(seen), in_vmem(own_c), in_vmem(oth_c), own_h, oth_h)


def x_body(parts, out, total, rest):
    for t in range(ROWS // LANE):
        at = slice(t * LANE, (t + 1) * LANE)
        tile = (parts[0, :, at].astype(f32) + parts[1, :, at].astype(f32)) + (
            parts[2, :, at].astype(f32) + parts[3, :, at].astype(f32)
        )
        total[t] = tile
        rest[at, 0:REST] = tile[4 * STRIPE :, :].T
    rest[ROWS:, 0:REST] = jnp.zeros((8, REST), f32)
    lane = lane_iota(STRIPE)
    for j in range(4):
        for z in range(8):
            at = j * PART + z * OWN
            last = roll(rest[at : at + STRIPE], 4 * OWN)
            acc = jnp.where(lane >= 4 * OWN, last, 0.0)
            for q in range(4):
                acc = put(acc, lambda k: total[k, q * STRIPE : (q + 1) * STRIPE], at, q * OWN, OWN)
            out[j * 8 + z] = acc.astype(bf16)


def x_sum(parts):
    return pl.pallas_call(
        x_body,
        out_shape=pltpu.VMEM((32, STRIPE, LANE), bf16),
        in_specs=[IN_VMEM],
        out_specs=IN_VMEM,
        scratch_shapes=[
            pltpu.VMEM((ROWS // LANE, COLS, LANE), f32),
            pltpu.VMEM((ROWS + 8, LANE), f32),
        ],
        name="x_sum",
    )(in_vmem(parts))


def z_body(parts, master, grad, copies):
    sums = [parts[z].astype(f32) for z in range(32)]
    while len(sums) > 1:
        sums = [a + b for a, b in zip(sums[::2], sums[1::2])]
    grad[...] = sums[0]
    new = (master[...] - 0.1 * sums[0]).astype(bf16)
    for d in range(32):
        copies[d] = new


def z_sum(parts, master):
    return pl.pallas_call(
        z_body,
        out_shape=(
            pltpu.VMEM((STRIPE, LANE), f32),
            pltpu.VMEM((32, STRIPE, LANE), bf16),
        ),
        in_specs=[IN_VMEM, IN_VMEM],
        out_specs=(IN_VMEM, IN_VMEM),
        name="z_sum",
    )(in_vmem(parts), in_vmem(master))


def rows_body(parts, out, wide, rest):
    for d in range(32):
        piece = parts[d].astype(f32)
        wide[d] = piece
        rest[d * OWN : (d + 1) * OWN, :] = roll(piece, -4 * OWN)[:OWN]
    for t in range(ROWS // LANE):
        at = slice(t * LANE, (t + 1) * LANE)
        for q in range(4):
            acc = jnp.zeros((STRIPE, LANE), f32)
            for d in range(32):
                lo = max(d * OWN, t * LANE)
                hi = min((d + 1) * OWN, (t + 1) * LANE)
                if lo < hi:
                    acc = put(acc, lambda k: wide[d], q * OWN + lo - d * OWN, lo - t * LANE, hi - lo)
            out[q * STRIPE : (q + 1) * STRIPE, at] = acc.astype(bf16)
        out[4 * STRIPE :, at] = rest[at, :].T[:REST].astype(bf16)


def row_block(parts):
    return pl.pallas_call(
        rows_body,
        out_shape=pltpu.VMEM((COLS, ROWS), bf16),
        in_specs=[IN_VMEM],
        out_specs=IN_VMEM,
        scratch_shapes=[
            pltpu.VMEM((32, STRIPE, LANE), f32),
            pltpu.VMEM((ROWS, LANE), f32),
        ],
        name="row_block",
    )(in_vmem(parts))


def pack(master):
    stripes = master[:, : 4 * STRIPE].reshape(OWN, 4, STRIPE).transpose(2, 1, 0).reshape(STRIPE, 4 * OWN)
    rest = jnp.pad(master[:, 4 * STRIPE :], ((0, STRIPE - OWN), (0, 0)))
    return jnp.concatenate([stripes, rest], axis=1)


def unpack(grad):
    stripes = grad[:, : 4 * OWN].reshape(STRIPE, 4, OWN).transpose(2, 1, 0).reshape(OWN, 4 * STRIPE)
    return jnp.concatenate([stripes, grad[:OWN, 4 * OWN :]], axis=1)


def in_vmem(array):
    return pltpu.with_memory_space_constraint(array, pltpu.VMEM)


def exchange(array, axis):
    return lax.all_to_all(array, axis, split_axis=0, concat_axis=0, tiled=True)


def shards(hidden, cotangent, rewards, groups, lengths, master):
    swap = [(0, 1), (1, 0)]
    cot = cotangent.T
    mine = jnp.stack([rewards, groups, lengths])
    chip = lax.all_gather(mine, CORE)
    other = chip[0] + chip[1] - mine
    plane = lax.all_gather(chip[:, :2], X)
    line = plane.transpose(2, 0, 1, 3).reshape(64)
    copies = jnp.broadcast_to(jnp.pad(line, (0, 64)), (32, LANE))
    copies, later_hidden, later_cot = lax.optimization_barrier((copies, hidden, cot))
    seen = exchange(copies, (ZH, ZL))
    other_hidden = lax.ppermute(later_hidden, CORE, swap)
    other_cot = lax.ppermute(later_cot, CORE, swap)
    core = lax.axis_index(CORE).astype(jnp.int32)
    scal = jnp.concatenate([core[None], jnp.stack([mine, other], axis=1).reshape(24)])
    parts = grad_parts(scal, seen, cot, other_cot, hidden, other_hidden)
    parts = x_sum(exchange(parts, X))
    grad, copies = z_sum(exchange(parts, (ZH, ZL)), pack(master[0]))
    block = row_block(exchange(copies, (X, ZL)))
    rollout = lax.all_gather(block, TP)
    rollout = rollout.reshape(4 * COLS, ROWS).T
    return (unpack(grad)[None], rollout[None])


def solution(mesh):
    torus = Mesh(
        mesh.devices.reshape(4, 8, 4, 2, mesh.shape["tp"]),
        (X, ZL, ZH, CORE, TP),
    )
    placed = (
        P(DP_FSDP, None),
        P(DP_FSDP, TP),
        P(DP_FSDP),
        P(DP_FSDP),
        P(DP_FSDP),
        P(FSDP, DP, TP),
    )
    return jax.shard_map(
        shards,
        mesh=torus,
        in_specs=placed,
        out_specs=(P(FSDP, DP, TP), P(FSDP, None, None)),
        check_vma=False,
    )
```

time: 206 us -> 177 us (0.86)
  blocking collectives: 84.4 us -> 44.1 us
  waiting for transfers between devices: 49.8 us -> 75.7 us
  starting transfers between devices: 47.8 us -> 40.8 us
  Pallas kernels: 15 us -> 8.95 us
    all_to_all x3, waiting for transfers between devices: 49.8 us -> 75.7 us  [exchange(): return lax.all_to_all(array, axis, split_axis=0, concat_axis=0, tiled=True)]
    all_to_all x2 -> x1, blocking collectives: 34.7 us -> 16.8 us  [exchange(): return lax.all_to_all(array, axis, split_axis=0, concat_axis=0, tiled=True)]
    all_gather x1 -> x0, blocking collectives: 13.1 us -> none  [shards(): plane = lax.all_gather(line, X)]
    all_gather x1, blocking collectives: 11.3 us -> 1.83 us  [shards(): chip = lax.all_gather(mine, CORE)]
    all_to_all x3, starting transfers between devices: 43.9 us -> 36.5 us  [exchange(): return lax.all_to_all(array, axis, split_axis=0, concat_axis=0, tiled=True)]
    pallas_call x5 -> x4, Pallas kernels: 15 us -> 8.95 us  [the longest x1 6.35 us: grad_parts(): pl.pallas_call(grad_body, out_shape=pltpu.VMEM((4, COLS, ROWS), bf16), gr...]
  transfers between devices with their start and end apart: 5 -> 5, of which waited for: 3 -> 3; matrix products, arithmetic and copies ran while one was open for 3% -> 2% of each run, Pallas kernels for 0% -> 0%
where the time goes in v2:
time: 177 us; the launch traced here: 176 us
  waiting for transfers between devices  75.7 us (43%)
  blocking collectives  44.1 us (25%)
  starting transfers between devices  40.8 us (23%)
  Pallas kernels  8.95 us (5%)
  local copies, waits for them, and re-layouts  3.98 us (2%)
  other arithmetic  2.05 us (1%)
    all_to_all x3, waiting for transfers between devices, exchange(): return lax.all_to_all(array, axis, split_axis=0, concat_axis=0, tiled=True)  75.7 us
    all_to_all x3, starting transfers between devices, exchange(): return lax.all_to_all(array, axis, split_axis=0, concat_axis=0, tiled=True)  36.5 us
    all_to_all x1, blocking collectives, exchange(): return lax.all_to_all(array, axis, split_axis=0, concat_axis=0, tiled=True)  16.8 us
    all_gather x1, blocking collectives, shards(): rollout = lax.all_gather(block, TP)  14.3 us
    all_gather x1, blocking collectives, shards(): plane = lax.all_gather(chip[:, :2], X)  11.1 us
    pallas_call x1, Pallas kernels, grad_parts(): pl.pallas_call(grad_body, out_shape=pltpu.VMEM((4, COLS, ROWS), bf16), gr...  6.35 us
  transfers between devices with their start and end apart: 5, of which 3 were waited for; matrix products, arithmetic and copies ran while one was open for 2% of the time, Pallas kernels for 0%

profile of v2, /device:TPU:8, one launch (start us, length us, event | category | flops | bytes accessed | tf_op | source)
XLA Modules:
  0.0 176.4 jit_solution(11360962805575807171)
XLA Ops:
  0.6 0.7 fusion.3
  1.3 1.8 %all-gather.3 = s32[2,3,4]{2,1,0:T(4,128)S(1)} all-gather(s32[1,3,4]{2,1,0:T(4,128)S(1)} %get-tuple-element.17), channel_id=2, replica_groups=mesh['x'=4,'z_lo'=8,'z_hi'=4,'core'=2,'tp'=4] {'core'}, dimensions={0}, use_global_device_ids=true | all-gather | bytes 144 | tf_op jit(solution)/shard_map/all_gather | solution.py:234
  3.2 11.1 %all-gather.1 = s32[8,2,4]{2,1,0:T(2,128)S(1)} all-gather(s32[2,2,4]{2,1,0:T(2,128)S(1)} %slice.34), channel_id=3, replica_groups=mesh['x'=4,'z_lo'=8,'z_hi'=4,'core'=2,'tp'=4] {'x'}, dimensions={0}, use_global_device_ids=true | all-gather | bytes 320 | tf_op jit(solution)/shard_map/all_gather | solution.py:236
  14.3 0.1 reshape.91
  14.4 0.6 broadcast_in_dim.13
  15.0 1.9 %collective-permute-start.1 = (bf16[512,7168]{1,0:T(8,128)(2,1)}, bf16[512,7168]{1,0:T(8,128)(2,1)}, u32[]{:S(2)}, u32[]{:S(2)}) collective-permute-start(bf16[512,7168]{1,0:T(8,128)(2,1)} %own_h.1), channel_id=1, source_target_pairs={{0,4},{4,0},{1,5},{5,1},{2,6},{6,2},{3,7},{7,3},{8,12},{12,8},{9,1... | collective-permute-start | bytes 22020104 | tf_op jit(solution)/shard_map/ppermute | solution.py:241
  16.9 2.4 %collective-permute-start = (bf16[144,512]{1,0:T(8,128)(2,1)}, bf16[144,512]{1,0:T(8,128)(2,1)S(1)}, u32[]{:S(2)}, u32[]{:S(2)}) collective-permute-start(bf16[144,512]{1,0:T(8,128)(2,1)} %bitcast.38), channel_id=1, source_target_pairs={{0,4},{4,0},{1,5},{5,1},{2,6},{6,2},{3,7},{7,3},{8,12},{12,8},{9,1... | collective-permute-start | bytes 442376 | tf_op jit(solution)/shard_map/ppermute | solution.py:242
  19.4 28.7 %all-to-all-start = ((s32[32,1,128]{2,1,0:T(1,128)}), s32[32,1,128]{2,1,0:T(1,128)S(1)}, u32[]{:S(2)}, u32[]{:S(2)}) async-start(s32[32,1,128]{2,1,0:T(1,128)} %bitcast.16), calls=%async_computation | async-start | bytes 32768 | tf_op jit(solution)/shard_map/all_to_all | solution.py:227
  48.1 0.7 fusion.1
  48.8 0.1 reshape.90
  48.9 0.6 pad_add_fusion.2.scal
  49.5 21.0 %all-to-all-done = s32[32,1,128]{2,1,0:T(1,128)S(1)} async-done(((s32[32,1,128]{2,1,0:T(1,128)}), s32[32,1,128]{2,1,0:T(1,128)S(1)}, u32[]{:S(2)}, u32[]{:S(2)}) %all-to-all-start) | async-done | bytes 16416 | tf_op jit(solution)/shard_map/all_to_all | solution.py:227
  70.5 0.9 copy-done
  71.4 6.4 %grad_parts.1 = bf16[4,144,896]{2,1,0:T(8,128)(2,1)S(1)} custom-call(s32[25]{0:T(128)} %pad_add_fusion.2.scal, s32[32,128]{1,0:T(8,128)S(1)} %bitcast.40, bf16[144,512]{1,0:T(8,128)(2,1)S(1)} %bitcast.39, bf16[144,512]{1,0:T(8,128)(2,1)S(1)} %collective-permute-done.oth_c, bf16[512,7168]{1,0:T(8,128)(2,1)} %own_h.1, ...), custom_call_target="tpu_custom_call" | custom-call | tf_op jit(solution)/shard_map/grad_parts/pallas_call | solution.py:97
  77.7 16.8 %all_to_all.26.parts = bf16[4,144,896]{2,1,0:T(8,128)(2,1)S(1)} all-to-all(bf16[4,144,896]{2,1,0:T(8,128)(2,1)S(1)} %grad_parts.1), channel_id=1, replica_groups=mesh['x'=4,'z_lo'=8,'z_hi'=4,'core'=2,'tp'=4] {'x'}, dimensions={0} | all-to-all | bytes 2064384 | tf_op jit(solution)/shard_map/all_to_all | solution.py:227
  94.6 1.3 x_sum.1
  95.9 3.9 %all-to-all-start.2 = ((bf16[32,32,128]{2,1,0:T(8,128)(2,1)}), bf16[32,32,128]{2,1,0:T(8,128)(2,1)S(1)}, u32[]{:S(2)}, u32[]{:S(2)}) async-start(bf16[32,32,128]{2,1,0:T(8,128)(2,1)} %x_sum.1), calls=%async_computation.2 | async-start | bytes 524288 | tf_op jit(solution)/shard_map/all_to_all | solution.py:227
  99.8 0.1 reshape.92
  99.9 0.1 copy.38
  100.0 0.1 reshape.93
  100.1 0.1 select_maximum_fusion.master
  100.2 40.1 %all-to-all-done.2.parts = bf16[32,32,128]{2,1,0:T(8,128)(2,1)S(1)} async-done(((bf16[32,32,128]{2,1,0:T(8,128)(2,1)}), bf16[32,32,128]{2,1,0:T(8,128)(2,1)S(1)}, u32[]{:S(2)}, u32[]{:S(2)}) %all-to-all-start.2) | async-done | bytes 262176 | tf_op jit(solution)/shard_map/all_to_all | solution.py:227
  140.2 0.8 z_sum.1
  141.0 3.9 %all-to-all-start.3 = ((bf16[32,32,128]{2,1,0:T(8,128)(2,1)}), bf16[32,32,128]{2,1,0:T(8,128)(2,1)S(1)}, u32[]{:S(2)}, u32[]{:S(2)}) async-start(bf16[32,32,128]{2,1,0:T(8,128)(2,1)} %get-tuple-element.11), calls=%async_computation.3 | async-start | bytes 524288 | tf_op jit(solution)/shard_map/all_to_all | solution.py:227
  144.9 0.1 reshape.94
  145.0 0.1 copy.39
  145.2 0.1 reshape.95
  145.3 0.6 copy.40
  145.9 14.7 %all-to-all-done.3.parts = bf16[32,32,128]{2,1,0:T(8,128)(2,1)S(1)} async-done(((bf16[32,32,128]{2,1,0:T(8,128)(2,1)}), bf16[32,32,128]{2,1,0:T(8,128)(2,1)S(1)}, u32[]{:S(2)}, u32[]{:S(2)}) %all-to-all-start.3) | async-done | bytes 262176 | tf_op jit(solution)/shard_map/all_to_all | solution.py:227
  160.6 0.5 row_block.1
  161.1 14.3 %all-gather.2 = bf16[576,896]{1,0:T(8,128)(2,1)S(1)} all-gather(bf16[144,896]{1,0:T(8,128)(2,1)S(1)} %row_block.1), channel_id=4, replica_groups=mesh['x'=4,'z_lo'=8,'z_hi'=4,'core'=2,'tp'=4] {'tp'}, dimensions={0}, use_global_device_ids=true | all-gather | bytes 1290240 | tf_op jit(solution)/shard_map/all_gather | solution.py:249
  175.5 1.0 copy.45
  (15 shorter events, 0.1 us)
Async XLA Ops:
  15.0 55.4 %collective-permute-start.1 = (bf16[512,7168]{1,0:T(8,128)(2,1)}, bf16[512,7168]{1,0:T(8,128)(2,1)}, u32[]{:S(2)}, u32[]{:S(2)}) collective-permute-start(bf16[512,7168]{1,0:T(8,128)(2,1)} %own_h.1), channel_id=1, source_target_pairs={{0,4},{4,0},{1,5},{5,1},{2,6},{6,2},{3,7},{7,3},{8,12},{12,8},{9,1... | collective-permute-start | bytes 22020104 | tf_op jit(solution)/shard_map/ppermute | solution.py:241
  16.9 53.5 %collective-permute-start = (bf16[144,512]{1,0:T(8,128)(2,1)}, bf16[144,512]{1,0:T(8,128)(2,1)S(1)}, u32[]{:S(2)}, u32[]{:S(2)}) collective-permute-start(bf16[144,512]{1,0:T(8,128)(2,1)} %bitcast.38), channel_id=1, source_target_pairs={{0,4},{4,0},{1,5},{5,1},{2,6},{6,2},{3,7},{7,3},{8,12},{12,8},{9,1... | collective-permute-start | bytes 442376 | tf_op jit(solution)/shard_map/ppermute | solution.py:242
  19.4 51.1 %all-to-all-start = ((s32[32,1,128]{2,1,0:T(1,128)}), s32[32,1,128]{2,1,0:T(1,128)S(1)}, u32[]{:S(2)}, u32[]{:S(2)}) async-start(s32[32,1,128]{2,1,0:T(1,128)} %bitcast.16), calls=%async_computation | async-start | bytes 32768 | tf_op jit(solution)/shard_map/all_to_all | solution.py:227
  70.5 0.9 copy-start
  71.4 28.4 %copy-start.1 = (f32[1,28,144]{2,0,1:T(1,128)S(1)}, f32[1,28,144]{2,0,1:T(1,128)}, u32[]{:S(2)}) copy-start(f32[1,28,144]{2,0,1:T(1,128)} %param.11) | copy-start | bytes 48388
  95.9 44.4 %all-to-all-start.2 = ((bf16[32,32,128]{2,1,0:T(8,128)(2,1)}), bf16[32,32,128]{2,1,0:T(8,128)(2,1)S(1)}, u32[]{:S(2)}, u32[]{:S(2)}) async-start(bf16[32,32,128]{2,1,0:T(8,128)(2,1)} %x_sum.1), calls=%async_computation.2 | async-start | bytes 524288 | tf_op jit(solution)/shard_map/all_to_all | solution.py:227
  141.0 19.6 %all-to-all-start.3 = ((bf16[32,32,128]{2,1,0:T(8,128)(2,1)}), bf16[32,32,128]{2,1,0:T(8,128)(2,1)S(1)}, u32[]{:S(2)}, u32[]{:S(2)}) async-start(bf16[32,32,128]{2,1,0:T(8,128)(2,1)} %get-tuple-element.11), calls=%async_computation.3 | async-start | bytes 524288 | tf_op jit(solution)/shard_map/all_to_all | solution.py:227

commit v3 on v2

--- a/solution.py
+++ b/solution.py
@@ -8,10 +8,10 @@
 
 
 GROUP = 16
-X, ZL, ZH, CORE, TP = "x", "z_lo", "z_hi", "core", "tp"
-DP = (X, ZL)
+X, ZA, ZB, ZH, CORE, TP = "x", "z_half", "z_quad", "z_hi", "core", "tp"
+DP = (X, ZA, ZB)
 FSDP = (ZH, CORE)
-DP_FSDP = (X, ZL, ZH, CORE)
+DP_FSDP = (X, ZA, ZB, ZH, CORE)
 
 ROWS = 896
 COLS = 144
@@ -102,7 +102,7 @@
             grid=(4,),
             in_specs=[
                 IN_VMEM,
-                IN_VMEM,
+                whole(own_c.shape),
                 IN_VMEM,
                 half,
                 half,
@@ -116,7 +116,7 @@
         ),
         compiler_params=pltpu.CompilerParams(dimension_semantics=("arbitrary",)),
         name="grad_parts",
-    )(scal, in_vmem(seen), in_vmem(own_c), in_vmem(oth_c), own_h, oth_h)
+    )(scal, in_vmem(seen), own_c, in_vmem(oth_c), own_h, oth_h)
 
 
 def x_body(parts, out, total, rest):
@@ -136,7 +136,8 @@
             acc = jnp.where(lane >= 4 * OWN, last, 0.0)
             for q in range(4):
                 acc = put(acc, lambda k: total[k, q * STRIPE : (q + 1) * STRIPE], at, q * OWN, OWN)
-            out[j * 8 + z] = acc.astype(bf16)
+            half, quad = divmod(z, 4)
+            out[quad * 8 + j * 2 + half] = acc.astype(bf16)
 
 
 def x_sum(parts):
@@ -153,32 +154,58 @@
     )(in_vmem(parts))
 
 
-def z_body(parts, master, grad, copies):
-    sums = [parts[z].astype(f32) for z in range(32)]
-    while len(sums) > 1:
-        sums = [a + b for a, b in zip(sums[::2], sums[1::2])]
-    grad[...] = sums[0]
-    new = (master[...] - 0.1 * sums[0]).astype(bf16)
-    for d in range(32):
-        copies[d] = new
-
-
-def z_sum(parts, master):
+def quad_body(parts, out):
+    for p in range(8):
+        total = (parts[p].astype(f32) + parts[8 + p].astype(f32)) + (
+            parts[16 + p].astype(f32) + parts[24 + p].astype(f32)
+        )
+        j, half = divmod(p, 2)
+        for to in range(2):
+            out[j * 4 + to * 2 + half] = total.astype(bf16)
+
+
+def quad_sum(parts):
+    return pl.pallas_call(
+        quad_body,
+        out_shape=pltpu.VMEM((16, STRIPE, LANE), bf16),
+        in_specs=[IN_VMEM],
+        out_specs=IN_VMEM,
+        name="quad_sum",
+    )(in_vmem(parts))
+
+
+def z_body(half, parts, mine, other, grad, copies):
+    for p in range(2):
+        total = [parts[2 * k + p].astype(f32) for k in range(8)]
+        while len(total) > 1:
+            total = [a + b for a, b in zip(total[::2], total[1::2])]
+        own = half[0] == p
+        new = (jnp.where(own, mine[...], other[...]) - 0.1 * total[0]).astype(bf16)
+        for d in range(16):
+            copies[2 * d + p] = new
+
+        @pl.when(own)
+        def _():
+            grad[...] = total[0]
+
+
+def z_sum(half, parts, mine, other):
     return pl.pallas_call(
         z_body,
         out_shape=(
             pltpu.VMEM((STRIPE, LANE), f32),
             pltpu.VMEM((32, STRIPE, LANE), bf16),
         ),
-        in_specs=[IN_VMEM, IN_VMEM],
+        in_specs=[pl.BlockSpec(memory_space=pltpu.SMEM), IN_VMEM, IN_VMEM, IN_VMEM],
         out_specs=(IN_VMEM, IN_VMEM),
         name="z_sum",
-    )(in_vmem(parts), in_vmem(master))
+    )(half, in_vmem(parts), in_vmem(mine), in_vmem(other))
 
 
 def rows_body(parts, out, wide, rest):
     for d in range(32):
-        piece = parts[d].astype(f32)
+        x, half, quad = d // 8, d % 8 // 4, d % 4
+        piece = parts[(x * 4 + quad) * 2 + half].astype(f32)
         wide[d] = piece
         rest[d * OWN : (d + 1) * OWN, :] = roll(piece, -4 * OWN)[:OWN]
     for t in range(ROWS // LANE):
@@ -236,16 +263,20 @@
     plane = lax.all_gather(chip[:, :2], X)
     line = plane.transpose(2, 0, 1, 3).reshape(64)
     copies = jnp.broadcast_to(jnp.pad(line, (0, 64)), (32, LANE))
-    copies, later_hidden, later_cot = lax.optimization_barrier((copies, hidden, cot))
-    seen = exchange(copies, (ZH, ZL))
+    copies, later_hidden, later_cot, later_master = lax.optimization_barrier((copies, hidden, cot, master))
+    packed = pack(later_master[0])
+    seen = exchange(copies, (ZH, ZA, ZB))
     other_hidden = lax.ppermute(later_hidden, CORE, swap)
     other_cot = lax.ppermute(later_cot, CORE, swap)
+    other_packed = lax.ppermute(packed, ZA, swap)
     core = lax.axis_index(CORE).astype(jnp.int32)
     scal = jnp.concatenate([core[None], jnp.stack([mine, other], axis=1).reshape(24)])
     parts = grad_parts(scal, seen, cot, other_cot, hidden, other_hidden)
     parts = x_sum(exchange(parts, X))
-    grad, copies = z_sum(exchange(parts, (ZH, ZL)), pack(master[0]))
-    block = row_block(exchange(copies, (X, ZL)))
+    parts = quad_sum(exchange(parts, ZB))
+    half = lax.axis_index(ZA).astype(jnp.int32)[None]
+    grad, copies = z_sum(half, exchange(parts, (ZH, ZA)), packed, other_packed)
+    block = row_block(exchange(copies, (X, ZB)))
     rollout = lax.all_gather(block, TP)
     rollout = rollout.reshape(4 * COLS, ROWS).T
     return (unpack(grad)[None], rollout[None])
@@ -253,8 +284,8 @@
 
 def solution(mesh):
     torus = Mesh(
-        mesh.devices.reshape(4, 8, 4, 2, mesh.shape["tp"]),
-        (X, ZL, ZH, CORE, TP),
+        mesh.devices.reshape(4, 2, 4, 4, 2, mesh.shape["tp"]),
+        (X, ZA, ZB, ZH, CORE, TP),
     )
     placed = (
         P(DP_FSDP, None),

time: 177 us -> 166 us (0.938)
  waiting for transfers between devices: 75.7 us -> 47.4 us
  blocking collectives: 44.1 us -> 53.3 us
  starting transfers between devices: 40.8 us -> 49.8 us
    all_to_all x3, waiting for transfers between devices: 75.7 us -> 43.2 us  [exchange(): return lax.all_to_all(array, axis, split_axis=0, concat_axis=0, tiled=True)]
    all_to_all x1 -> x2, blocking collectives: 16.8 us -> 26.3 us  [exchange(): return lax.all_to_all(array, axis, split_axis=0, concat_axis=0, tiled=True)]
    ppermute x0 -> x1, starting transfers between devices: none -> 7.82 us  [shards(): other_packed = lax.ppermute(packed, ZA, swap)]
    ppermute x0 -> x1, waiting for transfers between devices: none -> 4.17 us  [shards(): other_packed = lax.ppermute(packed, ZA, swap)]
  transfers between devices with their start and end apart: 5 -> 6, of which waited for: 3 -> 4; matrix products, arithmetic and copies ran while one was open for 2% -> 2% of each run, Pallas kernels for 0% -> 0%
where the time goes in v3:
time: 166 us; the launch traced here: 165 us
  blocking collectives  53.3 us (32%)
  starting transfers between devices  49.8 us (30%)
  waiting for transfers between devices  47.4 us (29%)
  Pallas kernels  8.96 us (5%)
  local copies, waits for them, and re-layouts  3.07 us (2%)
  other arithmetic  2.05 us (1%)
    all_to_all x3, waiting for transfers between devices, exchange(): return lax.all_to_all(array, axis, split_axis=0, concat_axis=0, tiled=True)  43.2 us
    all_to_all x3, starting transfers between devices, exchange(): return lax.all_to_all(array, axis, split_axis=0, concat_axis=0, tiled=True)  37.6 us
    all_to_all x2, blocking collectives, exchange(): return lax.all_to_all(array, axis, split_axis=0, concat_axis=0, tiled=True)  26.3 us
    all_gather x1, blocking collectives, shards(): rollout = lax.all_gather(block, TP)  14 us
    all_gather x1, blocking collectives, shards(): plane = lax.all_gather(chip[:, :2], X)  11.1 us
    ppermute x1, starting transfers between devices, shards(): other_packed = lax.ppermute(packed, ZA, swap)  7.82 us
    pallas_call x1, Pallas kernels, grad_parts(): pl.pallas_call(grad_body, out_shape=pltpu.VMEM((4, COLS, ROWS), bf16), gr...  6.39 us
    ppermute x1, waiting for transfers between devices, shards(): other_packed = lax.ppermute(packed, ZA, swap)  4.17 us
  transfers between devices with their start and end apart: 6, of which 4 were waited for; matrix products, arithmetic and copies ran while one was open for 2% of the time, Pallas kernels for 0%

profile of v3, /device:TPU:8, one launch (start us, length us, event | category | flops | bytes accessed | tf_op | source)
XLA Modules:
  0.0 165.4 jit_solution(4671866170128222127)
XLA Ops:
  0.6 0.7 fusion.3
  1.3 1.8 %all-gather.3 = s32[2,3,4]{2,1,0:T(4,128)S(1)} all-gather(s32[1,3,4]{2,1,0:T(4,128)S(1)} %get-tuple-element.19), channel_id=2, replica_groups=mesh['x'=4,'z_half'=2,'z_quad'=4,'z_hi'=4,'core'=2,'tp'=4] {'core'}, dimensions={0}, use_global_device_ids=true | all-gather | bytes 144 | tf_op jit(solution)/shard_map/all_gather | solution.py:261
  3.2 11.1 %all-gather.1 = s32[8,2,4]{2,1,0:T(2,128)S(1)} all-gather(s32[2,2,4]{2,1,0:T(2,128)S(1)} %slice.34), channel_id=3, replica_groups=mesh['x'=4,'z_half'=2,'z_quad'=4,'z_hi'=4,'core'=2,'tp'=4] {'x'}, dimensions={0}, use_global_device_ids=true | all-gather | bytes 320 | tf_op jit(solution)/shard_map/all_gather | solution.py:263
  14.3 0.1 reshape.91
  14.4 0.6 broadcast_in_dim.17
  15.0 1.9 %collective-permute-start.1 = (bf16[512,7168]{1,0:T(8,128)(2,1)}, bf16[512,7168]{1,0:T(8,128)(2,1)}, u32[]{:S(2)}, u32[]{:S(2)}) collective-permute-start(bf16[512,7168]{1,0:T(8,128)(2,1)} %own_h.1), channel_id=1, source_target_pairs={{0,4},{4,0},{1,5},{5,1},{2,6},{6,2},{3,7},{7,3},{8,12},{12,8},{9,1... | collective-permute-start | bytes 22020104 | tf_op jit(solution)/shard_map/ppermute | solution.py:269
  16.9 2.4 %collective-permute-start = (bf16[144,512]{1,0:T(8,128)(2,1)}, bf16[144,512]{1,0:T(8,128)(2,1)S(1)}, u32[]{:S(2)}, u32[]{:S(2)}) collective-permute-start(bf16[144,512]{1,0:T(8,128)(2,1)} %bitcast.44), channel_id=1, source_target_pairs={{0,4},{4,0},{1,5},{5,1},{2,6},{6,2},{3,7},{7,3},{8,12},{12,8},{9,1... | collective-permute-start | bytes 442376 | tf_op jit(solution)/shard_map/ppermute | solution.py:270
  19.4 28.7 %all-to-all-start = ((s32[32,1,128]{2,1,0:T(1,128)}), s32[32,1,128]{2,1,0:T(1,128)S(1)}, u32[]{:S(2)}, u32[]{:S(2)}) async-start(s32[32,1,128]{2,1,0:T(1,128)} %bitcast.17), calls=%async_computation | async-start | bytes 32768 | tf_op jit(solution)/shard_map/all_to_all | solution.py:254
  48.1 0.7 fusion.1
  48.9 0.6 pad_add_fusion.2.scal
  49.5 21.0 %all-to-all-done = s32[32,1,128]{2,1,0:T(1,128)S(1)} async-done(((s32[32,1,128]{2,1,0:T(1,128)}), s32[32,1,128]{2,1,0:T(1,128)S(1)}, u32[]{:S(2)}, u32[]{:S(2)}) %all-to-all-start) | async-done | bytes 16416 | tf_op jit(solution)/shard_map/all_to_all | solution.py:254
  70.5 6.4 %grad_parts.1 = bf16[4,144,896]{2,1,0:T(8,128)(2,1)S(1)} custom-call(s32[25]{0:T(128)} %pad_add_fusion.2.scal, s32[32,128]{1,0:T(8,128)S(1)} %bitcast.39, bf16[144,512]{1,0:T(8,128)(2,1)} %bitcast.45, bf16[144,512]{1,0:T(8,128)(2,1)S(1)} %collective-permute-done.oth_c, bf16[512,7168]{1,0:T(8,128)(2,1)} %own_h.1, bf16[512,7168]{1,0:T(8,128)(2,1)} %collective-permute-done.1.oth_h), custom_call_target="tpu_custom_call" | custom-call | tf_op jit(solution)/shard_map/grad_parts/pallas_call | solution.py:97
  76.9 16.8 %all_to_all.31.parts = bf16[4,144,896]{2,1,0:T(8,128)(2,1)S(1)} all-to-all(bf16[4,144,896]{2,1,0:T(8,128)(2,1)S(1)} %grad_parts.1), channel_id=1, replica_groups=mesh['x'=4,'z_half'=2,'z_quad'=4,'z_hi'=4,'core'=2,'tp'=4] {'x'}, dimensions={0} | all-to-all | bytes 2064384 | tf_op jit(solution)/shard_map/all_to_all | solution.py:254
  93.7 0.6 x_sum.1
  94.3 9.5 %all_to_all.32.parts = bf16[32,32,128]{2,1,0:T(8,128)(2,1)S(1)} all-to-all(bf16[32,32,128]{2,1,0:T(8,128)(2,1)S(1)} %x_sum.1), channel_id=1, replica_groups=mesh['x'=4,'z_half'=2,'z_quad'=4,'z_hi'=4,'core'=2,'tp'=4] {'z_quad'}, dimensions={0} | all-to-all | bytes 524288 | tf_op jit(solution)/shard_map/all_to_all | solution.py:254
  103.8 0.7 quad_sum.1
  104.5 3.8 %all-to-all-start.3 = ((bf16[16,32,128]{2,1,0:T(8,128)(2,1)}), bf16[16,32,128]{2,1,0:T(8,128)(2,1)S(1)}, u32[]{:S(2)}, u32[]{:S(2)}) async-start(bf16[16,32,128]{2,1,0:T(8,128)(2,1)} %quad_sum.1), calls=%async_computation.3 | async-start | bytes 262144 | tf_op jit(solution)/shard_map/all_to_all | solution.py:254
  108.4 0.1 copy.38
  108.5 0.1 reshape.93
  108.7 7.8 %collective-permute-start.2 = (f32[32,128]{1,0:T(8,128)S(1)}, f32[32,128]{1,0:T(8,128)S(1)}, u32[]{:S(2)}, u32[]{:S(2)}) collective-permute-start(f32[32,128]{1,0:T(8,128)S(1)} %select_maximum_fusion.mine), channel_id=1, source_target_pairs={{0,128},{128,0},{1,129},{129,1},{2,130},{130,2},{3,131},{131,3},{4... | collective-permute-start | bytes 49160 | tf_op jit(solution)/shard_map/ppermute | solution.py:271
  116.5 4.2 %collective-permute-done.2.other = f32[32,128]{1,0:T(8,128)S(1)} collective-permute-done((f32[32,128]{1,0:T(8,128)S(1)}, f32[32,128]{1,0:T(8,128)S(1)}, u32[]{:S(2)}, u32[]{:S(2)}) %collective-permute-start.2) | collective-permute-done | bytes 16416 | tf_op jit(solution)/shard_map/ppermute | solution.py:271
  120.7 14.1 %all-to-all-done.3.parts = bf16[16,32,128]{2,1,0:T(8,128)(2,1)S(1)} async-done(((bf16[16,32,128]{2,1,0:T(8,128)(2,1)}), bf16[16,32,128]{2,1,0:T(8,128)(2,1)S(1)}, u32[]{:S(2)}, u32[]{:S(2)}) %all-to-all-start.3) | async-done | bytes 131104 | tf_op jit(solution)/shard_map/all_to_all | solution.py:254
  134.8 0.8 z_sum.1
  135.6 5.1 %all-to-all-start.4 = ((bf16[32,32,128]{2,1,0:T(8,128)(2,1)}), bf16[32,32,128]{2,1,0:T(8,128)(2,1)S(1)}, u32[]{:S(2)}, u32[]{:S(2)}) async-start(bf16[32,32,128]{2,1,0:T(8,128)(2,1)} %get-tuple-element.13), calls=%async_computation.4 | async-start | bytes 524288 | tf_op jit(solution)/shard_map/all_to_all | solution.py:254
  140.7 0.1 reshape.94
  140.8 0.1 copy.39
  141.0 0.1 reshape.95
  141.1 0.6 copy.40
  141.7 8.1 %all-to-all-done.4.parts = bf16[32,32,128]{2,1,0:T(8,128)(2,1)S(1)} async-done(((bf16[32,32,128]{2,1,0:T(8,128)(2,1)}), bf16[32,32,128]{2,1,0:T(8,128)(2,1)S(1)}, u32[]{:S(2)}, u32[]{:S(2)}) %all-to-all-start.4) | async-done | bytes 262176 | tf_op jit(solution)/shard_map/all_to_all | solution.py:254
  149.8 0.5 row_block.1
  150.4 14.0 %all-gather.2 = bf16[576,896]{1,0:T(8,128)(2,1)S(1)} all-gather(bf16[144,896]{1,0:T(8,128)(2,1)S(1)} %row_block.1), channel_id=4, replica_groups=mesh['x'=4,'z_half'=2,'z_quad'=4,'z_hi'=4,'core'=2,'tp'=4] {'tp'}, dimensions={0}, use_global_device_ids=true | all-gather | bytes 1290240 | tf_op jit(solution)/shard_map/all_gather | solution.py:280
  164.4 1.0 copy.45
  (17 shorter events, 0.4 us)
Async XLA Ops:
  15.0 55.4 %collective-permute-start.1 = (bf16[512,7168]{1,0:T(8,128)(2,1)}, bf16[512,7168]{1,0:T(8,128)(2,1)}, u32[]{:S(2)}, u32[]{:S(2)}) collective-permute-start(bf16[512,7168]{1,0:T(8,128)(2,1)} %own_h.1), channel_id=1, source_target_pairs={{0,4},{4,0},{1,5},{5,1},{2,6},{6,2},{3,7},{7,3},{8,12},{12,8},{9,1... | collective-permute-start | bytes 22020104 | tf_op jit(solution)/shard_map/ppermute | solution.py:269
  16.9 53.5 %collective-permute-start = (bf16[144,512]{1,0:T(8,128)(2,1)}, bf16[144,512]{1,0:T(8,128)(2,1)S(1)}, u32[]{:S(2)}, u32[]{:S(2)}) collective-permute-start(bf16[144,512]{1,0:T(8,128)(2,1)} %bitcast.44), channel_id=1, source_target_pairs={{0,4},{4,0},{1,5},{5,1},{2,6},{6,2},{3,7},{7,3},{8,12},{12,8},{9,1... | collective-permute-start | bytes 442376 | tf_op jit(solution)/shard_map/ppermute | solution.py:270
  19.4 51.1 %all-to-all-start = ((s32[32,1,128]{2,1,0:T(1,128)}), s32[32,1,128]{2,1,0:T(1,128)S(1)}, u32[]{:S(2)}, u32[]{:S(2)}) async-start(s32[32,1,128]{2,1,0:T(1,128)} %bitcast.17), calls=%async_computation | async-start | bytes 32768 | tf_op jit(solution)/shard_map/all_to_all | solution.py:254
  70.5 37.8 %copy-start = (f32[1,28,144]{2,0,1:T(1,128)S(1)}, f32[1,28,144]{2,0,1:T(1,128)}, u32[]{:S(2)}) copy-start(f32[1,28,144]{2,0,1:T(1,128)} %param.11) | copy-start | bytes 48388
  104.5 30.4 %all-to-all-start.3 = ((bf16[16,32,128]{2,1,0:T(8,128)(2,1)}), bf16[16,32,128]{2,1,0:T(8,128)(2,1)S(1)}, u32[]{:S(2)}, u32[]{:S(2)}) async-start(bf16[16,32,128]{2,1,0:T(8,128)(2,1)} %quad_sum.1), calls=%async_computation.3 | async-start | bytes 262144 | tf_op jit(solution)/shard_map/all_to_all | solution.py:254
  108.7 12.0 %collective-permute-start.2 = (f32[32,128]{1,0:T(8,128)S(1)}, f32[32,128]{1,0:T(8,128)S(1)}, u32[]{:S(2)}, u32[]{:S(2)}) collective-permute-start(f32[32,128]{1,0:T(8,128)S(1)} %select_maximum_fusion.mine), channel_id=1, source_target_pairs={{0,128},{128,0},{1,129},{129,1},{2,130},{130,2},{3,131},{131,3},{4... | collective-permute-start | bytes 49160 | tf_op jit(solution)/shard_map/ppermute | solution.py:271
  135.6 14.2 %all-to-all-start.4 = ((bf16[32,32,128]{2,1,0:T(8,128)(2,1)}), bf16[32,32,128]{2,1,0:T(8,128)(2,1)S(1)}, u32[]{:S(2)}, u32[]{:S(2)}) async-start(bf16[32,32,128]{2,1,0:T(8,128)(2,1)} %get-tuple-element.13), calls=%async_computation.4 | async-start | bytes 524288 | tf_op jit(solution)/shard_map/all_to_all | solution.py:254

commit v4 on v3

--- a/solution.py
+++ b/solution.py
@@ -257,24 +257,27 @@
 def shards(hidden, cotangent, rewards, groups, lengths, master):
     swap = [(0, 1), (1, 0)]
     cot = cotangent.T
-    mine = jnp.stack([rewards, groups, lengths])
-    chip = lax.all_gather(mine, CORE)
-    other = chip[0] + chip[1] - mine
-    plane = lax.all_gather(chip[:, :2], X)
-    line = plane.transpose(2, 0, 1, 3).reshape(64)
-    copies = jnp.broadcast_to(jnp.pad(line, (0, 64)), (32, LANE))
-    copies, later_hidden, later_cot, later_master = lax.optimization_barrier((copies, hidden, cot, master))
-    packed = pack(later_master[0])
-    seen = exchange(copies, (ZH, ZA, ZB))
+    mine = jnp.concatenate([rewards, groups, lengths])
+    plane = lax.all_gather(mine, (X, CORE)).reshape(4, 2, 3, 4)
+    row = plane.transpose(2, 0, 1, 3).reshape(3, 32)
+    copies = jnp.broadcast_to(jnp.pad(row[:2].reshape(64), (0, 64)), (32, LANE))
+    copies, later_hidden, later_cot, later_master = lax.optimization_barrier((copies, hidden, cot, master[0]))
     other_hidden = lax.ppermute(later_hidden, CORE, swap)
     other_cot = lax.ppermute(later_cot, CORE, swap)
-    other_packed = lax.ppermute(packed, ZA, swap)
+    other_master = lax.ppermute(later_master, ZA, swap)
+    seen = exchange(copies, (ZH, ZA, ZB))
     core = lax.axis_index(CORE).astype(jnp.int32)
-    scal = jnp.concatenate([core[None], jnp.stack([mine, other], axis=1).reshape(24)])
+    chip = lax.dynamic_index_in_dim(plane, lax.axis_index(X), 0, keepdims=False)
+    other = chip[0] + chip[1] - mine.reshape(3, 4)
+    scal = jnp.concatenate([core[None], jnp.stack([mine.reshape(3, 4), other], axis=1).reshape(24)])
+    packed, other_packed = pack(later_master), pack(other_master)
+    half = lax.axis_index(ZA).astype(jnp.int32)[None]
+    seen, packed, other_packed, scal, half = lax.optimization_barrier(
+        (seen, packed, other_packed, scal, half)
+    )
     parts = grad_parts(scal, seen, cot, other_cot, hidden, other_hidden)
     parts = x_sum(exchange(parts, X))
     parts = quad_sum(exchange(parts, ZB))
-    half = lax.axis_index(ZA).astype(jnp.int32)[None]
     grad, copies = z_sum(half, exchange(parts, (ZH, ZA)), packed, other_packed)
     block = row_block(exchange(copies, (X, ZB)))
     rollout = lax.all_gather(block, TP)

time: 166 us -> 173 us (1.042)
  blocking collectives: 53.3 us -> 91.6 us
  waiting for transfers between devices: 47.4 us -> 18 us
  starting transfers between devices: 49.8 us -> 44.1 us
  local copies, waits for them, and re-layouts: 3.07 us -> 5.5 us
    all_to_all x2 -> x3, blocking collectives: 26.3 us -> 67.1 us  [exchange(): return lax.all_to_all(array, axis, split_axis=0, concat_axis=0, tiled=True)]
    all_to_all x3 -> x2, waiting for transfers between devices: 43.2 us -> 18 us  [exchange(): return lax.all_to_all(array, axis, split_axis=0, concat_axis=0, tiled=True)]
    all_gather x2 -> x0, blocking collectives: 13 us -> none  [the longest x1 11.1 us: shards(): plane = lax.all_gather(chip[:, :2], X)]
    unnamed x0 -> x1, blocking collectives: none -> 9.22 us
    all_to_all x3 -> x2, starting transfers between devices: 37.6 us -> 32.7 us  [exchange(): return lax.all_to_all(array, axis, split_axis=0, concat_axis=0, tiled=True)]
    ppermute x1, waiting for transfers between devices: 4.17 us -> 0.01 us  [shards(): other_master = lax.ppermute(later_master, ZA, swap)]
    unnamed x5, local copies, waits for them, and re-layouts: 1.61 us -> 3.63 us
  transfers between devices with their start and end apart: 6 -> 5, of which waited for: 4 -> 2; matrix products, arithmetic and copies ran while one was open for 2% -> 2% of each run, Pallas kernels for 0% -> 0%
where the time goes in v4:
time: 173 us; the launch traced here: 172 us
  blocking collectives  91.6 us (53%)
  starting transfers between devices  44.1 us (25%)
  waiting for transfers between devices  18 us (10%)
  Pallas kernels  8.18 us (5%)
  local copies, waits for them, and re-layouts  5.5 us (3%)
  other arithmetic  3.07 us (2%)
    all_to_all x3, blocking collectives, exchange(): return lax.all_to_all(array, axis, split_axis=0, concat_axis=0, tiled=True)  67.1 us
    all_to_all x2, starting transfers between devices, exchange(): return lax.all_to_all(array, axis, split_axis=0, concat_axis=0, tiled=True)  32.7 us
    all_to_all x2, waiting for transfers between devices, exchange(): return lax.all_to_all(array, axis, split_axis=0, concat_axis=0, tiled=True)  18 us
    all_gather x1, blocking collectives, shards(): rollout = lax.all_gather(block, TP)  15.3 us
    unnamed x1, blocking collectives  9.22 us
    ppermute x1, starting transfers between devices, shards(): other_master = lax.ppermute(later_master, ZA, swap)  7.61 us
    pallas_call x1, Pallas kernels, grad_parts(): pl.pallas_call(grad_body, out_shape=pltpu.VMEM((4, COLS, ROWS), bf16), gr...  6.26 us
    unnamed x5, local copies, waits for them, and re-layouts  3.63 us
  transfers between devices with their start and end apart: 5, of which 2 were waited for; matrix products, arithmetic and copies ran while one was open for 2% of the time, Pallas kernels for 0%

profile of v4, /device:TPU:8, one launch (start us, length us, event | category | flops | bytes accessed | tf_op | source)
XLA Modules:
  0.0 172.0 jit_solution(10319405629037301567)
XLA Ops:
  0.6 1.3 dynamic-slice
  2.6 0.9 add_dynamic-update-slice_fusion
  3.4 9.2 %all-reduce.3 = s32[96]{0:T(128)S(1)} all-reduce(s32[96]{0:T(128)S(1)} %add_dynamic-update-slice_fusion), channel_id=2, replica_groups=mesh['x'=4,'z_half'=2,'z_quad'=4,'z_hi'=4,'core'=2,'tp'=4] {'x','core'}, use_global_device_ids=true, to_apply=%add.3 | all-reduce | flops 96 | bytes 768
  12.7 0.1 reshape.108
  12.9 0.8 copy.27
  13.7 0.6 broadcast_in_dim.15
  14.3 1.9 %collective-permute-start.2 = (bf16[512,7168]{1,0:T(8,128)(2,1)}, bf16[512,7168]{1,0:T(8,128)(2,1)}, u32[]{:S(2)}, u32[]{:S(2)}) collective-permute-start(bf16[512,7168]{1,0:T(8,128)(2,1)} %own_h.1), channel_id=1, source_target_pairs={{0,4},{4,0},{1,5},{5,1},{2,6},{6,2},{3,7},{7,3},{8,12},{12,8},{9,1... | collective-permute-start | bytes 22020104 | tf_op jit(solution)/shard_map/ppermute | solution.py:265
  16.2 28.7 %all-to-all-start = ((s32[32,1,128]{2,1,0:T(1,128)}), s32[32,1,128]{2,1,0:T(1,128)S(1)}, u32[]{:S(2)}, u32[]{:S(2)}) async-start(s32[32,1,128]{2,1,0:T(1,128)} %bitcast.3), calls=%async_computation | async-start | bytes 32768 | tf_op jit(solution)/shard_map/all_to_all | solution.py:254
  44.9 7.6 %collective-permute-start = (f32[28,144]{1,0:T(8,128)S(1)}, f32[28,144]{1,0:T(8,128)S(1)}, u32[]{:S(2)}, u32[]{:S(2)}) collective-permute-start(f32[28,144]{1,0:T(8,128)S(1)} %bitcast.30), channel_id=1, source_target_pairs={{0,128},{128,0},{1,129},{129,1},{2,130},{130,2},{3,131},{131,3},{4... | collective-permute-start | bytes 48392 | tf_op jit(solution)/shard_map/ppermute | solution.py:267
  52.5 1.9 %collective-permute-start.1 = (bf16[144,512]{1,0:T(8,128)(2,1)}, bf16[144,512]{1,0:T(8,128)(2,1)S(1)}, u32[]{:S(2)}, u32[]{:S(2)}) collective-permute-start(bf16[144,512]{1,0:T(8,128)(2,1)} %bitcast.28), channel_id=1, source_target_pairs={{0,4},{4,0},{1,5},{5,1},{2,6},{6,2},{3,7},{7,3},{8,12},{12,8},{9,1... | collective-permute-start | bytes 442376 | tf_op jit(solution)/shard_map/ppermute | solution.py:266
  54.5 0.7 add_subtract_fusion
  55.2 0.7 pad_add_fusion
  56.1 0.1 copy.21
  56.2 0.1 reshape.111
  56.4 0.6 pad_add_fusion.1.scal
  57.1 0.1 copy.22
  57.2 0.1 reshape.113
  57.4 9.9 %all-to-all-done = s32[32,1,128]{2,1,0:T(1,128)S(1)} async-done(((s32[32,1,128]{2,1,0:T(1,128)}), s32[32,1,128]{2,1,0:T(1,128)S(1)}, u32[]{:S(2)}, u32[]{:S(2)}) %all-to-all-start) | async-done | bytes 16416 | tf_op jit(solution)/shard_map/all_to_all | solution.py:254
  67.3 6.3 %grad_parts.1 = bf16[4,144,896]{2,1,0:T(8,128)(2,1)S(1)} custom-call(s32[25]{0:T(128)} %pad_add_fusion.1.scal, s32[32,128]{1,0:T(8,128)S(1)} %bitcast.22, bf16[144,512]{1,0:T(8,128)(2,1)} %bitcast.29, bf16[144,512]{1,0:T(8,128)(2,1)S(1)} %collective-permute-done.1.oth_c, bf16[512,7168]{1,0:T(8,128)(2,1)} %own_h.1, bf16[512,7168]{1,0:T(8,128)(2,1)} %collective-permute-done.2.oth_h), custom_call_target="tpu_custom_call" | custom-call | tf_op jit(solution)/shard_map/grad_parts/pallas_call | solution.py:97
  73.6 16.8 %all_to_all.32.parts = bf16[4,144,896]{2,1,0:T(8,128)(2,1)S(1)} all-to-all(bf16[4,144,896]{2,1,0:T(8,128)(2,1)S(1)} %grad_parts.1), channel_id=1, replica_groups=mesh['x'=4,'z_half'=2,'z_quad'=4,'z_hi'=4,'core'=2,'tp'=4] {'x'}, dimensions={0} | all-to-all | bytes 2064384 | tf_op jit(solution)/shard_map/all_to_all | solution.py:254
  90.4 0.6 x_sum.1
  91.0 9.5 %all_to_all.33.parts = bf16[32,32,128]{2,1,0:T(8,128)(2,1)S(1)} all-to-all(bf16[32,32,128]{2,1,0:T(8,128)(2,1)S(1)} %x_sum.1), channel_id=1, replica_groups=mesh['x'=4,'z_half'=2,'z_quad'=4,'z_hi'=4,'core'=2,'tp'=4] {'z_quad'}, dimensions={0} | all-to-all | bytes 524288 | tf_op jit(solution)/shard_map/all_to_all | solution.py:254
  100.6 40.7 %all_to_all.34.parts = bf16[16,32,128]{2,1,0:T(8,128)(2,1)S(1)} all-to-all(bf16[16,32,128]{2,1,0:T(8,128)(2,1)S(1)} %quad_sum.1), channel_id=1, replica_groups=mesh['x'=4,'z_half'=2,'z_quad'=4,'z_hi'=4,'core'=2,'tp'=4] {'z_hi','z_ha..., dimensions={0} | all-to-all | bytes 262144 | tf_op jit(solution)/shard_map/all_to_all | solution.py:254
  141.3 0.8 z_sum.1
  142.0 3.9 %all-to-all-start.4 = ((bf16[32,32,128]{2,1,0:T(8,128)(2,1)}), bf16[32,32,128]{2,1,0:T(8,128)(2,1)S(1)}, u32[]{:S(2)}, u32[]{:S(2)}) async-start(bf16[32,32,128]{2,1,0:T(8,128)(2,1)} %get-tuple-element.23), calls=%async_computation.4 | async-start | bytes 524288 | tf_op jit(solution)/shard_map/all_to_all | solution.py:254
  146.2 0.1 copy.23
  146.3 0.1 reshape.116
  146.4 0.6 copy.24
  147.0 8.1 %all-to-all-done.4.parts = bf16[32,32,128]{2,1,0:T(8,128)(2,1)S(1)} async-done(((bf16[32,32,128]{2,1,0:T(8,128)(2,1)}), bf16[32,32,128]{2,1,0:T(8,128)(2,1)S(1)}, u32[]{:S(2)}, u32[]{:S(2)}) %all-to-all-start.4) | async-done | bytes 262176 | tf_op jit(solution)/shard_map/all_to_all | solution.py:254
  155.1 0.5 row_block.1
  155.7 15.3 %all-gather.1 = bf16[576,896]{1,0:T(8,128)(2,1)S(1)} all-gather(bf16[144,896]{1,0:T(8,128)(2,1)S(1)} %row_block.1), channel_id=3, replica_groups=mesh['x'=4,'z_half'=2,'z_quad'=4,'z_hi'=4,'core'=2,'tp'=4] {'tp'}, dimensions={0}, use_global_device_ids=true | all-gather | bytes 1290240 | tf_op jit(solution)/shard_map/all_gather | solution.py:283
  171.0 1.0 copy.30
  (22 shorter events, 0.8 us)
Async XLA Ops:
  14.3 53.1 %collective-permute-start.2 = (bf16[512,7168]{1,0:T(8,128)(2,1)}, bf16[512,7168]{1,0:T(8,128)(2,1)}, u32[]{:S(2)}, u32[]{:S(2)}) collective-permute-start(bf16[512,7168]{1,0:T(8,128)(2,1)} %own_h.1), channel_id=1, source_target_pairs={{0,4},{4,0},{1,5},{5,1},{2,6},{6,2},{3,7},{7,3},{8,12},{12,8},{9,1... | collective-permute-start | bytes 22020104 | tf_op jit(solution)/shard_map/ppermute | solution.py:265
  16.2 51.1 %all-to-all-start = ((s32[32,1,128]{2,1,0:T(1,128)}), s32[32,1,128]{2,1,0:T(1,128)S(1)}, u32[]{:S(2)}, u32[]{:S(2)}) async-start(s32[32,1,128]{2,1,0:T(1,128)} %bitcast.3), calls=%async_computation | async-start | bytes 32768 | tf_op jit(solution)/shard_map/all_to_all | solution.py:254
  44.9 12.1 %collective-permute-start = (f32[28,144]{1,0:T(8,128)S(1)}, f32[28,144]{1,0:T(8,128)S(1)}, u32[]{:S(2)}, u32[]{:S(2)}) collective-permute-start(f32[28,144]{1,0:T(8,128)S(1)} %bitcast.30), channel_id=1, source_target_pairs={{0,128},{128,0},{1,129},{129,1},{2,130},{130,2},{3,131},{131,3},{4... | collective-permute-start | bytes 48392 | tf_op jit(solution)/shard_map/ppermute | solution.py:267
  52.5 14.8 %collective-permute-start.1 = (bf16[144,512]{1,0:T(8,128)(2,1)}, bf16[144,512]{1,0:T(8,128)(2,1)S(1)}, u32[]{:S(2)}, u32[]{:S(2)}) collective-permute-start(bf16[144,512]{1,0:T(8,128)(2,1)} %bitcast.28), channel_id=1, source_target_pairs={{0,4},{4,0},{1,5},{5,1},{2,6},{6,2},{3,7},{7,3},{8,12},{12,8},{9,1... | collective-permute-start | bytes 442376 | tf_op jit(solution)/shard_map/ppermute | solution.py:266
  142.0 13.1 %all-to-all-start.4 = ((bf16[32,32,128]{2,1,0:T(8,128)(2,1)}), bf16[32,32,128]{2,1,0:T(8,128)(2,1)S(1)}, u32[]{:S(2)}, u32[]{:S(2)}) async-start(bf16[32,32,128]{2,1,0:T(8,128)(2,1)} %get-tuple-element.23), calls=%async_computation.4 | async-start | bytes 524288 | tf_op jit(solution)/shard_map/all_to_all | solution.py:254

commit v5 on v4

--- a/solution.py
+++ b/solution.py
@@ -20,6 +20,7 @@
 STRIPE = 32
 REST = 16
 LANE = 128
+INFO = 12
 IN_VMEM = pl.BlockSpec(memory_space=pltpu.VMEM)
 f32 = jnp.float32
 bf16 = jnp.bfloat16
@@ -47,25 +48,27 @@
     return acc
 
 
-def grad_body(scal, seen, own_c, oth_c, own_h, oth_h, out, w_own, w_oth, edge):
+def grad_body(place_at, x_at, info, seen, own_c, oth_c, own_h, oth_h, out, w_own, w_oth, edge):
     step = pl.program_id(0)
 
     @pl.when(step == 0)
     def _():
-        seen_r = seen[:, 0:32].astype(f32)
-        seen_g = seen[:, 32:64]
+        lane = lane_iota(seen.shape[0])
+        rewards = jnp.where((lane < 8 * INFO) & (lane % INFO < 4), seen[...], 0).astype(f32)
+        labels = roll(seen[...], -4)
         pos = lax.broadcasted_iota(jnp.int32, (1, LANE), 1)
         for s in range(8):
-            hit = seen_g == scal[9 + s]
-            total = jnp.sum(jnp.where(hit, seen_r, 0.0), axis=(0, 1), keepdims=True)
-            square = jnp.sum(jnp.where(hit, seen_r * seen_r, 0.0), axis=(0, 1), keepdims=True)
+            core = place_at[0] % 2 if s < 4 else 1 - place_at[0] % 2
+            base = (x_at[0] * 2 + core) * INFO + s % 4
+            reward, label, length = info[base], info[base + 4], info[base + 8]
+            mates = jnp.where(labels == label, rewards, 0.0)
+            total = jnp.sum(mates, axis=(0, 1), keepdims=True)
+            square = jnp.sum(mates * mates, axis=(0, 1), keepdims=True)
             mean = total / GROUP
             var = square / GROUP - mean * mean
-            reward = jnp.full((1, 1), scal[1 + s], jnp.int32).astype(f32)
-            adv = (reward - mean) / jnp.sqrt(var + 1.0)
-            size = jnp.full((1, 1), scal[17 + s], jnp.int32).astype(f32)
-            live = jnp.where(pos < scal[17 + s], 1.0, 0.0)
-            scale = adv * live / size
+            adv = (jnp.full((1, 1), reward, jnp.int32).astype(f32) - mean) / jnp.sqrt(var + 1.0)
+            live = jnp.where(pos < length, 1.0, 0.0)
+            scale = adv * live / jnp.full((1, 1), length, jnp.int32).astype(f32)
             src, dst = (own_c, w_own) if s < 4 else (oth_c, w_oth)
             at = (s % 4) * LANE
             dst[:, at : at + LANE] = (src[:, at : at + LANE].astype(f32) * scale).astype(bf16)
@@ -90,15 +93,15 @@
         pl.when(step == j)(lambda j=j: place(j))
 
 
-def grad_parts(scal, seen, own_c, oth_c, own_h, oth_h):
+def grad_parts(place_at, x_at, info, seen, own_c, oth_c, own_h, oth_h):
     tokens = own_h.shape[0]
-    half = pl.BlockSpec((tokens, ROWS), lambda j, scal: (0, 2 * j + scal[0]))
-    whole = lambda shape: pl.BlockSpec(shape, lambda j, scal: (0,) * len(shape))
+    half = pl.BlockSpec((tokens, ROWS), lambda j, place, x, info: (0, 2 * j + place[0] % 2))
+    whole = lambda shape: pl.BlockSpec(shape, lambda j, place, x, info: (0,) * len(shape))
     return pl.pallas_call(
         grad_body,
         out_shape=pltpu.VMEM((4, COLS, ROWS), bf16),
         grid_spec=pltpu.PrefetchScalarGridSpec(
-            num_scalar_prefetch=1,
+            num_scalar_prefetch=3,
             grid=(4,),
             in_specs=[
                 IN_VMEM,
@@ -116,7 +119,7 @@
         ),
         compiler_params=pltpu.CompilerParams(dimension_semantics=("arbitrary",)),
         name="grad_parts",
-    )(scal, in_vmem(seen), own_c, in_vmem(oth_c), own_h, oth_h)
+    )(place_at, x_at, info, in_vmem(seen), own_c, in_vmem(oth_c), own_h, oth_h)
 
 
 def x_body(parts, out, total, rest):
@@ -174,32 +177,50 @@
     )(in_vmem(parts))
 
 
-def z_body(half, parts, mine, other, grad, copies):
+def packed(master, wide, tall):
+    wide[0:OWN, 0:COLS] = master[:, 0, :]
+    tall[0:OWN] = wide[0:OWN, 0:LANE]
+    stripes = tall[...].T
+    lane = lane_iota(STRIPE)
+    acc = jnp.where(lane >= 4 * OWN, roll(wide[:, LANE:], 4 * OWN), 0.0)
+    for q in range(4):
+        acc = put(acc, lambda k: stripes[q * STRIPE : (q + 1) * STRIPE], 0, q * OWN, OWN)
+    return acc
+
+
+def z_body(place_at, parts, mine, other, grad, copies, wide, tall):
+    wide[...] = jnp.zeros(wide.shape, f32)
+    tall[...] = jnp.zeros(tall.shape, f32)
+    masters = packed(mine, wide, tall), packed(other, wide, tall)
     for p in range(2):
         total = [parts[2 * k + p].astype(f32) for k in range(8)]
         while len(total) > 1:
             total = [a + b for a, b in zip(total[::2], total[1::2])]
-        own = half[0] == p
-        new = (jnp.where(own, mine[...], other[...]) - 0.1 * total[0]).astype(bf16)
+        own = place_at[0] // 2 == p
+        new = (jnp.where(own, *masters) - 0.1 * total[0]).astype(bf16)
         for d in range(16):
             copies[2 * d + p] = new
 
         @pl.when(own)
         def _():
-            grad[...] = total[0]
-
-
-def z_sum(half, parts, mine, other):
+            for q in range(4):
+                tall[q * STRIPE : (q + 1) * STRIPE] = roll(total[0], -q * OWN)
+            grad[:, 0, 0:LANE] = tall[...].T[:OWN]
+            grad[:, 0, LANE:COLS] = roll(total[0], -4 * OWN)[:OWN, : COLS - LANE]
+
+
+def z_sum(place_at, parts, mine, other):
     return pl.pallas_call(
         z_body,
         out_shape=(
-            pltpu.VMEM((STRIPE, LANE), f32),
+            pltpu.VMEM((OWN, 1, COLS), f32),
             pltpu.VMEM((32, STRIPE, LANE), bf16),
         ),
         in_specs=[pl.BlockSpec(memory_space=pltpu.SMEM), IN_VMEM, IN_VMEM, IN_VMEM],
         out_specs=(IN_VMEM, IN_VMEM),
+        scratch_shapes=[pltpu.VMEM((STRIPE, 2 * LANE), f32), pltpu.VMEM((LANE, LANE), f32)],
         name="z_sum",
-    )(half, in_vmem(parts), in_vmem(mine), in_vmem(other))
+    )(place_at, in_vmem(parts), in_vmem(mine), in_vmem(other))
 
 
 def rows_body(parts, out, wide, rest):
@@ -235,17 +256,6 @@
     )(in_vmem(parts))
 
 
-def pack(master):
-    stripes = master[:, : 4 * STRIPE].reshape(OWN, 4, STRIPE).transpose(2, 1, 0).reshape(STRIPE, 4 * OWN)
-    rest = jnp.pad(master[:, 4 * STRIPE :], ((0, STRIPE - OWN), (0, 0)))
-    return jnp.concatenate([stripes, rest], axis=1)
-
-
-def unpack(grad):
-    stripes = grad[:, : 4 * OWN].reshape(STRIPE, 4, OWN).transpose(2, 1, 0).reshape(OWN, 4 * STRIPE)
-    return jnp.concatenate([stripes, grad[:OWN, 4 * OWN :]], axis=1)
-
-
 def in_vmem(array):
     return pltpu.with_memory_space_constraint(array, pltpu.VMEM)
 
@@ -257,32 +267,29 @@
 def shards(hidden, cotangent, rewards, groups, lengths, master):
     swap = [(0, 1), (1, 0)]
     cot = cotangent.T
+    core, x, half = (lax.axis_index(name).astype(jnp.int32) for name in (CORE, X, ZA))
+    place_at = half * 2 + core
+    base = (x * 2 + place_at % 2) * INFO
     mine = jnp.concatenate([rewards, groups, lengths])
-    plane = lax.all_gather(mine, (X, CORE)).reshape(4, 2, 3, 4)
-    row = plane.transpose(2, 0, 1, 3).reshape(3, 32)
-    copies = jnp.broadcast_to(jnp.pad(row[:2].reshape(64), (0, 64)), (32, LANE))
-    copies, later_hidden, later_cot, later_master = lax.optimization_barrier((copies, hidden, cot, master[0]))
+    info = lax.dynamic_update_slice(jnp.zeros(LANE, jnp.int32), mine, (base,))
+    info = lax.psum(info, (X, CORE))
+    copies = jnp.broadcast_to(info, (32, LANE))
+    copies, later_hidden, later_cot, info = lax.optimization_barrier((copies, hidden, cot, info))
     other_hidden = lax.ppermute(later_hidden, CORE, swap)
     other_cot = lax.ppermute(later_cot, CORE, swap)
+    seen = exchange(copies, (ZH, ZA, ZB))
+    parts = grad_parts(place_at[None], x[None], info, seen, cot, other_cot, hidden, other_hidden)
+    parts, later_master = lax.optimization_barrier((parts, master.transpose(1, 0, 2)))
+    parts = exchange(parts, X)
     other_master = lax.ppermute(later_master, ZA, swap)
-    seen = exchange(copies, (ZH, ZA, ZB))
-    core = lax.axis_index(CORE).astype(jnp.int32)
-    chip = lax.dynamic_index_in_dim(plane, lax.axis_index(X), 0, keepdims=False)
-    other = chip[0] + chip[1] - mine.reshape(3, 4)
-    scal = jnp.concatenate([core[None], jnp.stack([mine.reshape(3, 4), other], axis=1).reshape(24)])
-    packed, other_packed = pack(later_master), pack(other_master)
-    half = lax.axis_index(ZA).astype(jnp.int32)[None]
-    seen, packed, other_packed, scal, half = lax.optimization_barrier(
-        (seen, packed, other_packed, scal, half)
-    )
-    parts = grad_parts(scal, seen, cot, other_cot, hidden, other_hidden)
-    parts = x_sum(exchange(parts, X))
-    parts = quad_sum(exchange(parts, ZB))
-    grad, copies = z_sum(half, exchange(parts, (ZH, ZA)), packed, other_packed)
+    parts, later_master, other_master = lax.optimization_barrier((parts, later_master, other_master))
+    parts = quad_sum(exchange(x_sum(parts), ZB))
+    grad, copies = z_sum(place_at[None], exchange(parts, (ZH, ZA)), later_master, other_master)
     block = row_block(exchange(copies, (X, ZB)))
+    block, grad = lax.optimization_barrier((block, grad))
     rollout = lax.all_gather(block, TP)
     rollout = rollout.reshape(4 * COLS, ROWS).T
-    return (unpack(grad)[None], rollout[None])
+    return (grad.transpose(1, 0, 2), rollout[None])
 
 
 def solution(mesh):

time: 173 us -> 164 us (0.948)
  blocking collectives: 91.6 us -> 127 us
  starting transfers between devices: 44.1 us -> 10.2 us
  waiting for transfers between devices: 18 us -> 11.6 us
  other arithmetic: 3.07 us -> 0.86 us
    all_to_all x3 -> x4, blocking collectives: 67.1 us -> 103 us  [exchange(): return lax.all_to_all(array, axis, split_axis=0, concat_axis=0, tiled=True)]
    all_to_all x2 -> x1, starting transfers between devices: 32.7 us -> 3.52 us  [exchange(): return lax.all_to_all(array, axis, split_axis=0, concat_axis=0, tiled=True)]
    all_to_all x2 -> x1, waiting for transfers between devices: 18 us -> 3.81 us  [exchange(): return lax.all_to_all(array, axis, split_axis=0, concat_axis=0, tiled=True)]
    psum x0 -> x1, blocking collectives: none -> 9.22 us  [shards(): info = lax.psum(info, (X, CORE))]
    unnamed x1 -> x0, blocking collectives: 9.22 us -> none
    ppermute x1, waiting for transfers between devices: 0.01 us -> 7.82 us  [shards(): other_master = lax.ppermute(later_master, ZA, swap)]
    ppermute x1, starting transfers between devices: 7.61 us -> 2.34 us  [shards(): other_master = lax.ppermute(later_master, ZA, swap)]
    unnamed x5 -> x8, local copies, waits for them, and re-layouts: 3.63 us -> 4.53 us
  transfers between devices with their start and end apart: 5 -> 4, of which waited for: 2 -> 2; matrix products, arithmetic and copies ran while one was open for 2% -> 0% of each run, Pallas kernels for 0% -> 0%
where the time goes in v5:
time: 164 us; the launch traced here: 163 us
  blocking collectives  127 us (77%)
  waiting for transfers between devices  11.6 us (7%)
  starting transfers between devices  10.2 us (6%)
  Pallas kernels  8.7 us (5%)
  local copies, waits for them, and re-layouts  4.54 us (3%)
    all_to_all x4, blocking collectives, exchange(): return lax.all_to_all(array, axis, split_axis=0, concat_axis=0, tiled=True)  103 us
    all_gather x1, blocking collectives, shards(): rollout = lax.all_gather(block, TP)  14 us
    psum x1, blocking collectives, shards(): info = lax.psum(info, (X, CORE))  9.22 us
    ppermute x1, waiting for transfers between devices, shards(): other_master = lax.ppermute(later_master, ZA, swap)  7.82 us
    pallas_call x1, Pallas kernels, grad_parts(): pl.pallas_call(grad_body, out_shape=pltpu.VMEM((4, COLS, ROWS), bf16), gr...  7.19 us
    unnamed x8, local copies, waits for them, and re-layouts  4.53 us
    all_to_all x1, waiting for transfers between devices, exchange(): return lax.all_to_all(array, axis, split_axis=0, concat_axis=0, tiled=True)  3.81 us
    all_to_all x1, starting transfers between devices, exchange(): return lax.all_to_all(array, axis, split_axis=0, concat_axis=0, tiled=True)  3.52 us
  transfers between devices with their start and end apart: 4, of which 2 were waited for; matrix products, arithmetic and copies ran while one was open for 0% of the time, Pallas kernels for 0%

profile of v5, /device:TPU:8, one launch (start us, length us, event | category | flops | bytes accessed | tf_op | source)
XLA Modules:
  0.0 163.3 jit_solution(9921063182458932504)
XLA Ops:
  0.7 0.9 add_dynamic-update-slice_fusion
  1.5 9.2 %psum.7.info = s32[128]{0:T(128)S(1)} all-reduce(s32[128]{0:T(128)S(1)} %add_dynamic-update-slice_fusion), channel_id=1, replica_groups=mesh['x'=4,'z_half'=2,'z_quad'=4,'z_hi'=4,'core'=2,'tp'=4] {'x','core'}, use_global_device_ids=true, to_apply=%region_0.1 | all-reduce | flops 128 | bytes 1024 | tf_op jit(solution)/shard_map/psum | solution.py:275
  10.7 0.0 copy-start.2
  10.8 1.9 %collective-permute-start.1 = (bf16[512,7168]{1,0:T(8,128)(2,1)}, bf16[512,7168]{1,0:T(8,128)(2,1)S(1)}, u32[]{:S(2)}, u32[]{:S(2)}) collective-permute-start(bf16[512,7168]{1,0:T(8,128)(2,1)} %own_h.1), channel_id=1, source_target_pairs={{0,4},{4,0},{1,5},{5,1},{2,6},{6,2},{3,7},{7,3},{8,12},{12,8},{9,1... | collective-permute-start | bytes 22020104 | tf_op jit(solution)/shard_map/ppermute | solution.py:278
  12.7 2.4 %collective-permute-start = (bf16[144,512]{1,0:T(8,128)(2,1)}, bf16[144,512]{1,0:T(8,128)(2,1)S(1)}, u32[]{:S(2)}, u32[]{:S(2)}) collective-permute-start(bf16[144,512]{1,0:T(8,128)(2,1)} %bitcast.15), channel_id=1, source_target_pairs={{0,4},{4,0},{1,5},{5,1},{2,6},{6,2},{3,7},{7,3},{8,12},{12,8},{9,1... | collective-permute-start | bytes 442376 | tf_op jit(solution)/shard_map/ppermute | solution.py:279
  15.1 50.9 %all_to_all.31 = s32[32,1,128]{2,1,0:T(1,128)S(1)} all-to-all(s32[32,1,128]{2,1,0:T(1,128)S(1)} %bitcast.17), channel_id=1, replica_groups=mesh['x'=4,'z_half'=2,'z_quad'=4,'z_hi'=4,'core'=2,'tp'=4] {'z_hi','z_ha..., dimensions={0} | all-to-all | bytes 32768 | tf_op jit(solution)/shard_map/all_to_all | solution.py:264
  66.0 0.0 collective-permute-done.oth_c
  66.0 0.0 collective-permute-done.1.oth_h
  66.0 0.0 copy-start.1
  66.0 3.0 %copy-done.1 = bf16[512,7168]{1,0:T(8,128)(2,1)} copy-done((bf16[512,7168]{1,0:T(8,128)(2,1)}, bf16[512,7168]{1,0:T(8,128)(2,1)S(1)}, u32[]{:S(2)}) %copy-start.1) | copy-done | bytes 7340056
  69.0 0.0 copy-done.2
  69.0 0.0 copy-start
  69.0 7.2 %grad_parts.1 = bf16[4,144,896]{2,1,0:T(8,128)(2,1)} custom-call(s32[1]{0:T(128)} %bitcast.place_at, s32[1]{0:T(128)} %bitcast.1.x_at, s32[128]{0:T(128)} %copy-done.2, s32[32,128]{1,0:T(8,128)S(1)} %bitcast.11, bf16[144,512]{1,0:T(8,128)(2,1)} %bitcast.16, bf16[144,512]{1,0:T(8,128)(2,1)S(1)} %collective-permute-done.oth_c, bf16[512,7168]{1,0:T(8,128)(2,1)} %own_h.1, ...), custom_call_target="tpu_custom_call" | custom-call | tf_op jit(solution)/shard_map/grad_parts/pallas_call | solution.py:100
  76.2 3.5 %all-to-all-start.1 = ((bf16[4,144,896]{2,1,0:T(8,128)(2,1)}), bf16[4,144,896]{2,1,0:T(8,128)(2,1)S(1)}, u32[]{:S(2)}, u32[]{:S(2)}) async-start(bf16[4,144,896]{2,1,0:T(8,128)(2,1)} %grad_parts.1), calls=%async_computation.1 | async-start | bytes 2064384 | tf_op jit(solution)/shard_map/all_to_all | solution.py:264
  79.7 0.0 copy-done
  79.7 2.3 %collective-permute-start.2 = (f32[28,1,144]{2,1,0:T(1,128)S(1)}, f32[28,1,144]{2,1,0:T(1,128)S(1)}, u32[]{:S(2)}, u32[]{:S(2)}) collective-permute-start(f32[28,1,144]{2,1,0:T(1,128)S(1)} %bitcast.12), channel_id=1, source_target_pairs={{0,128},{128,0},{1,129},{129,1},{2,130},{130,2},{3,131},{131,3},{4... | collective-permute-start | bytes 48392 | tf_op jit(solution)/shard_map/ppermute | solution.py:284
  82.1 7.8 %collective-permute-done.2.other = f32[28,1,144]{2,1,0:T(1,128)S(1)} collective-permute-done((f32[28,1,144]{2,1,0:T(1,128)S(1)}, f32[28,1,144]{2,1,0:T(1,128)S(1)}, u32[]{:S(2)}, u32[]{:S(2)}) %collective-permute-start.2) | collective-permute-done | bytes 16160 | tf_op jit(solution)/shard_map/ppermute | solution.py:284
  89.9 3.8 %all-to-all-done.1.parts = bf16[4,144,896]{2,1,0:T(8,128)(2,1)S(1)} async-done(((bf16[4,144,896]{2,1,0:T(8,128)(2,1)}), bf16[4,144,896]{2,1,0:T(8,128)(2,1)S(1)}, u32[]{:S(2)}, u32[]{:S(2)}) %all-to-all-start.1) | async-done | bytes 1032224 | tf_op jit(solution)/shard_map/all_to_all | solution.py:264
  93.7 0.6 x_sum.1
  94.3 9.5 %all_to_all.32.parts = bf16[32,32,128]{2,1,0:T(8,128)(2,1)S(1)} all-to-all(bf16[32,32,128]{2,1,0:T(8,128)(2,1)S(1)} %x_sum.1), channel_id=1, replica_groups=mesh['x'=4,'z_half'=2,'z_quad'=4,'z_hi'=4,'core'=2,'tp'=4] {'z_quad'}, dimensions={0} | all-to-all | bytes 524288 | tf_op jit(solution)/shard_map/all_to_all | solution.py:264
  103.8 30.0 %all_to_all.33.parts = bf16[16,32,128]{2,1,0:T(8,128)(2,1)S(1)} all-to-all(bf16[16,32,128]{2,1,0:T(8,128)(2,1)S(1)} %quad_sum.1), channel_id=1, replica_groups=mesh['x'=4,'z_half'=2,'z_quad'=4,'z_hi'=4,'core'=2,'tp'=4] {'z_hi','z_ha..., dimensions={0} | all-to-all | bytes 262144 | tf_op jit(solution)/shard_map/all_to_all | solution.py:264
  133.8 0.3 z_sum.1
  134.2 13.0 %all_to_all.34.parts = bf16[32,32,128]{2,1,0:T(8,128)(2,1)S(1)} all-to-all(bf16[32,32,128]{2,1,0:T(8,128)(2,1)S(1)} %get-tuple-element.24), channel_id=1, replica_groups=mesh['x'=4,'z_half'=2,'z_quad'=4,'z_hi'=4,'core'=2,'tp'=4] {'x','z_quad'}, dimensions={0} | all-to-all | bytes 524288 | tf_op jit(solution)/shard_map/all_to_all | solution.py:264
  147.2 0.5 row_block.1
  147.7 0.6 copy.10
  148.3 14.0 %all-gather = bf16[576,896]{1,0:T(8,128)(2,1)S(1)} all-gather(bf16[144,896]{1,0:T(8,128)(2,1)S(1)} %row_block.1), channel_id=2, replica_groups=mesh['x'=4,'z_half'=2,'z_quad'=4,'z_hi'=4,'core'=2,'tp'=4] {'tp'}, dimensions={0}, use_global_device_ids=true | all-gather | bytes 1290240 | tf_op jit(solution)/shard_map/all_gather | solution.py:290
  162.4 1.0 copy.11
  (3 shorter events, 0.0 us)
Async XLA Ops:
  10.7 58.3 %copy-start.2 = (s32[128]{0:T(128)}, s32[128]{0:T(128)S(1)}, u32[]{:S(2)}) copy-start(s32[128]{0:T(128)S(1)} %psum.7.info) | copy-start | bytes 1540
  10.8 55.3 %collective-permute-start.1 = (bf16[512,7168]{1,0:T(8,128)(2,1)}, bf16[512,7168]{1,0:T(8,128)(2,1)S(1)}, u32[]{:S(2)}, u32[]{:S(2)}) collective-permute-start(bf16[512,7168]{1,0:T(8,128)(2,1)} %own_h.1), channel_id=1, source_target_pairs={{0,4},{4,0},{1,5},{5,1},{2,6},{6,2},{3,7},{7,3},{8,12},{12,8},{9,1... | collective-permute-start | bytes 22020104 | tf_op jit(solution)/shard_map/ppermute | solution.py:278
  12.7 53.4 %collective-permute-start = (bf16[144,512]{1,0:T(8,128)(2,1)}, bf16[144,512]{1,0:T(8,128)(2,1)S(1)}, u32[]{:S(2)}, u32[]{:S(2)}) collective-permute-start(bf16[144,512]{1,0:T(8,128)(2,1)} %bitcast.15), channel_id=1, source_target_pairs={{0,4},{4,0},{1,5},{5,1},{2,6},{6,2},{3,7},{7,3},{8,12},{12,8},{9,1... | collective-permute-start | bytes 442376 | tf_op jit(solution)/shard_map/ppermute | solution.py:279
  66.0 3.0 %copy-start.1 = (bf16[512,7168]{1,0:T(8,128)(2,1)}, bf16[512,7168]{1,0:T(8,128)(2,1)S(1)}, u32[]{:S(2)}) copy-start(bf16[512,7168]{1,0:T(8,128)(2,1)S(1)} %collective-permute-done.1.oth_h) | copy-start | bytes 22020100
  69.0 10.7 %copy-start = (f32[1,28,144]{2,0,1:T(1,128)S(1)}, f32[1,28,144]{2,0,1:T(1,128)}, u32[]{:S(2)}) copy-start(f32[1,28,144]{2,0,1:T(1,128)} %param.11) | copy-start | bytes 48388
  76.2 17.5 %all-to-all-start.1 = ((bf16[4,144,896]{2,1,0:T(8,128)(2,1)}), bf16[4,144,896]{2,1,0:T(8,128)(2,1)S(1)}, u32[]{:S(2)}, u32[]{:S(2)}) async-start(bf16[4,144,896]{2,1,0:T(8,128)(2,1)} %grad_parts.1), calls=%async_computation.1 | async-start | bytes 2064384 | tf_op jit(solution)/shard_map/all_to_all | solution.py:264
  79.7 10.2 %collective-permute-start.2 = (f32[28,1,144]{2,1,0:T(1,128)S(1)}, f32[28,1,144]{2,1,0:T(1,128)S(1)}, u32[]{:S(2)}, u32[]{:S(2)}) collective-permute-start(f32[28,1,144]{2,1,0:T(1,128)S(1)} %bitcast.12), channel_id=1, source_target_pairs={{0,128},{128,0},{1,129},{129,1},{2,130},{130,2},{3,131},{131,3},{4... | collective-permute-start | bytes 48392 | tf_op jit(solution)/shard_map/ppermute | solution.py:284

commit v6 on v5

--- a/solution.py
+++ b/solution.py
@@ -74,7 +74,8 @@
             dst[:, at : at + LANE] = (src[:, at : at + LANE].astype(f32) * scale).astype(bf16)
 
     block = jnp.dot(w_own[...], own_h[...], preferred_element_type=f32)
-    block += jnp.dot(w_oth[...], oth_h[...], preferred_element_type=f32)
+    at = pl.multiple_of((2 * step + place_at[0] % 2) * ROWS, LANE)
+    block += jnp.dot(w_oth[...], oth_h[:, pl.ds(at, ROWS)], preferred_element_type=f32)
 
     def place(j):
         lo, hi = j * PART, (j + 1) * PART
@@ -108,7 +109,7 @@
                 whole(own_c.shape),
                 IN_VMEM,
                 half,
-                half,
+                IN_VMEM,
             ],
             out_specs=whole((4, COLS, ROWS)),
             scratch_shapes=[
@@ -117,9 +118,11 @@
                 pltpu.VMEM((4, COLS, LANE), f32),
             ],
         ),
-        compiler_params=pltpu.CompilerParams(dimension_semantics=("arbitrary",)),
+        compiler_params=pltpu.CompilerParams(
+            dimension_semantics=("arbitrary",), vmem_limit_bytes=24 << 20
+        ),
         name="grad_parts",
-    )(place_at, x_at, info, in_vmem(seen), own_c, in_vmem(oth_c), own_h, oth_h)
+    )(place_at, x_at, info, in_vmem(seen), in_hbm(own_c), in_vmem(oth_c), in_hbm(own_h), in_vmem(oth_h))
 
 
 def x_body(parts, out, total, rest):
@@ -258,6 +261,10 @@
 
 def in_vmem(array):
     return pltpu.with_memory_space_constraint(array, pltpu.VMEM)
+
+
+def in_hbm(array):
+    return pltpu.with_memory_space_constraint(array, pltpu.HBM)
 
 
 def exchange(array, axis):
@@ -287,9 +294,8 @@
     grad, copies = z_sum(place_at[None], exchange(parts, (ZH, ZA)), later_master, other_master)
     block = row_block(exchange(copies, (X, ZB)))
     block, grad = lax.optimization_barrier((block, grad))
-    rollout = lax.all_gather(block, TP)
-    rollout = rollout.reshape(4 * COLS, ROWS).T
-    return (grad.transpose(1, 0, 2), rollout[None])
+    rollout = lax.all_gather(block.T[None], TP, axis=2, tiled=True)
+    return (grad.transpose(1, 0, 2), rollout)
 
 
 def solution(mesh):

time: 164 us -> 160 us (0.976)
  local copies, waits for them, and re-layouts: 4.54 us -> 1.58 us
    unnamed x8 -> x4, local copies, waits for them, and re-layouts: 4.53 us -> 1.58 us
where the time goes in v6:
time: 160 us; the launch traced here: 159 us
  blocking collectives  127 us (79%)
  waiting for transfers between devices  11.6 us (7%)
  starting transfers between devices  10.2 us (6%)
  Pallas kernels  7.83 us (5%)
    all_to_all x4, blocking collectives, exchange(): return lax.all_to_all(array, axis, split_axis=0, concat_axis=0, tiled=True)  103 us
    all_gather x1, blocking collectives, shards(): rollout = lax.all_gather(block.T[None], TP, axis=2, tiled=True)  14 us
    psum x1, blocking collectives, shards(): info = lax.psum(info, (X, CORE))  9.22 us
    ppermute x1, waiting for transfers between devices, shards(): other_master = lax.ppermute(later_master, ZA, swap)  7.81 us
    pallas_call x1, Pallas kernels, grad_parts(): pl.pallas_call(grad_body, out_shape=pltpu.VMEM((4, COLS, ROWS), bf16), gr...  6.31 us
    all_to_all x1, waiting for transfers between devices, exchange(): return lax.all_to_all(array, axis, split_axis=0, concat_axis=0, tiled=True)  3.76 us
    all_to_all x1, starting transfers between devices, exchange(): return lax.all_to_all(array, axis, split_axis=0, concat_axis=0, tiled=True)  3.52 us
  transfers between devices with their start and end apart: 4, of which 2 were waited for; matrix products, arithmetic and copies ran while one was open for 0% of the time, Pallas kernels for 0%

profile of v6, /device:TPU:8, one launch (start us, length us, event | category | flops | bytes accessed | tf_op | source)
XLA Modules:
  0.0 159.4 jit_solution(13691697662579440355)
XLA Ops:
  0.7 0.9 add_dynamic-update-slice_fusion
  1.5 9.2 %psum.7.info = s32[128]{0:T(128)S(1)} all-reduce(s32[128]{0:T(128)S(1)} %add_dynamic-update-slice_fusion), channel_id=1, replica_groups=mesh['x'=4,'z_half'=2,'z_quad'=4,'z_hi'=4,'core'=2,'tp'=4] {'x','core'}, use_global_device_ids=true, to_apply=%region_0.1 | all-reduce | flops 128 | bytes 1024 | tf_op jit(solution)/shard_map/psum | solution.py:282
  10.8 1.9 %collective-permute-start.1 = (bf16[512,7168]{1,0:T(8,128)(2,1)}, bf16[512,7168]{1,0:T(8,128)(2,1)S(1)}, u32[]{:S(2)}, u32[]{:S(2)}) collective-permute-start(bf16[512,7168]{1,0:T(8,128)(2,1)} %own_h.1), channel_id=1, source_target_pairs={{0,4},{4,0},{1,5},{5,1},{2,6},{6,2},{3,7},{7,3},{8,12},{12,8},{9,1... | collective-permute-start | bytes 22020104 | tf_op jit(solution)/shard_map/ppermute | solution.py:285
  12.7 2.4 %collective-permute-start = (bf16[144,512]{1,0:T(8,128)(2,1)}, bf16[144,512]{1,0:T(8,128)(2,1)S(1)}, u32[]{:S(2)}, u32[]{:S(2)}) collective-permute-start(bf16[144,512]{1,0:T(8,128)(2,1)} %bitcast.15), channel_id=1, source_target_pairs={{0,4},{4,0},{1,5},{5,1},{2,6},{6,2},{3,7},{7,3},{8,12},{12,8},{9,1... | collective-permute-start | bytes 442376 | tf_op jit(solution)/shard_map/ppermute | solution.py:286
  15.1 50.9 %all_to_all.31 = s32[32,1,128]{2,1,0:T(1,128)S(1)} all-to-all(s32[32,1,128]{2,1,0:T(1,128)S(1)} %bitcast.17), channel_id=1, replica_groups=mesh['x'=4,'z_half'=2,'z_quad'=4,'z_hi'=4,'core'=2,'tp'=4] {'z_hi','z_ha..., dimensions={0} | all-to-all | bytes 32768 | tf_op jit(solution)/shard_map/all_to_all | solution.py:271
  66.0 0.0 collective-permute-done.oth_c
  66.0 0.0 collective-permute-done.1.oth_h
  66.0 0.0 copy-start
  66.0 6.3 %grad_parts.1 = bf16[4,144,896]{2,1,0:T(8,128)(2,1)} custom-call(s32[1]{0:T(128)} %bitcast.place_at, s32[1]{0:T(128)} %bitcast.1.x_at, s32[128]{0:T(128)S(1)} %psum.7.info, s32[32,128]{1,0:T(8,128)S(1)} %bitcast.11, bf16[144,512]{1,0:T(8,128)(2,1)} %bitcast.16, bf16[144,512]{1,0:T(8,128)(2,1)S(1)} %collective-permute-done.oth_c, bf16[512,7168]{1,0:T(8,128)(2,1)} %own_h.1, ...), custom_call_target="tpu_custom_call" | custom-call | tf_op jit(solution)/shard_map/grad_parts/pallas_call | solution.py:101
  72.4 3.5 %all-to-all-start.1 = ((bf16[4,144,896]{2,1,0:T(8,128)(2,1)}), bf16[4,144,896]{2,1,0:T(8,128)(2,1)S(1)}, u32[]{:S(2)}, u32[]{:S(2)}) async-start(bf16[4,144,896]{2,1,0:T(8,128)(2,1)} %grad_parts.1), calls=%async_computation.1 | async-start | bytes 2064384 | tf_op jit(solution)/shard_map/all_to_all | solution.py:271
  75.9 0.0 copy-done
  75.9 2.4 %collective-permute-start.2 = (f32[28,1,144]{2,1,0:T(1,128)S(1)}, f32[28,1,144]{2,1,0:T(1,128)S(1)}, u32[]{:S(2)}, u32[]{:S(2)}) collective-permute-start(f32[28,1,144]{2,1,0:T(1,128)S(1)} %bitcast.12), channel_id=1, source_target_pairs={{0,128},{128,0},{1,129},{129,1},{2,130},{130,2},{3,131},{131,3},{4... | collective-permute-start | bytes 48392 | tf_op jit(solution)/shard_map/ppermute | solution.py:291
  78.2 7.8 %collective-permute-done.2.other = f32[28,1,144]{2,1,0:T(1,128)S(1)} collective-permute-done((f32[28,1,144]{2,1,0:T(1,128)S(1)}, f32[28,1,144]{2,1,0:T(1,128)S(1)}, u32[]{:S(2)}, u32[]{:S(2)}) %collective-permute-start.2) | collective-permute-done | bytes 16160 | tf_op jit(solution)/shard_map/ppermute | solution.py:291
  86.1 3.8 %all-to-all-done.1.parts = bf16[4,144,896]{2,1,0:T(8,128)(2,1)S(1)} async-done(((bf16[4,144,896]{2,1,0:T(8,128)(2,1)}), bf16[4,144,896]{2,1,0:T(8,128)(2,1)S(1)}, u32[]{:S(2)}, u32[]{:S(2)}) %all-to-all-start.1) | async-done | bytes 1032224 | tf_op jit(solution)/shard_map/all_to_all | solution.py:271
  89.8 0.6 x_sum.1
  90.4 9.5 %all_to_all.32.parts = bf16[32,32,128]{2,1,0:T(8,128)(2,1)S(1)} all-to-all(bf16[32,32,128]{2,1,0:T(8,128)(2,1)S(1)} %x_sum.1), channel_id=1, replica_groups=mesh['x'=4,'z_half'=2,'z_quad'=4,'z_hi'=4,'core'=2,'tp'=4] {'z_quad'}, dimensions={0} | all-to-all | bytes 524288 | tf_op jit(solution)/shard_map/all_to_all | solution.py:271
  100.0 30.0 %all_to_all.33.parts = bf16[16,32,128]{2,1,0:T(8,128)(2,1)S(1)} all-to-all(bf16[16,32,128]{2,1,0:T(8,128)(2,1)S(1)} %quad_sum.1), channel_id=1, replica_groups=mesh['x'=4,'z_half'=2,'z_quad'=4,'z_hi'=4,'core'=2,'tp'=4] {'z_hi','z_ha..., dimensions={0} | all-to-all | bytes 262144 | tf_op jit(solution)/shard_map/all_to_all | solution.py:271
  129.9 0.3 z_sum.1
  130.3 12.9 %all_to_all.34.parts = bf16[32,32,128]{2,1,0:T(8,128)(2,1)S(1)} all-to-all(bf16[32,32,128]{2,1,0:T(8,128)(2,1)S(1)} %get-tuple-element.24), channel_id=1, replica_groups=mesh['x'=4,'z_half'=2,'z_quad'=4,'z_hi'=4,'core'=2,'tp'=4] {'x','z_quad'}, dimensions={0} | all-to-all | bytes 524288 | tf_op jit(solution)/shard_map/all_to_all | solution.py:271
  143.2 0.5 row_block.1
  143.8 0.6 copy.10
  144.4 14.0 %all-gather = bf16[896,576]{0,1:T(8,128)(2,1)S(1)} all-gather(bf16[896,144]{0,1:T(8,128)(2,1)S(1)} %bitcast.10), channel_id=2, replica_groups=mesh['x'=4,'z_half'=2,'z_quad'=4,'z_hi'=4,'core'=2,'tp'=4] {'tp'}, dimensions={1}, use_global_device_ids=true | all-gather | bytes 1290240 | tf_op jit(solution)/shard_map/all_gather | solution.py:297
  158.4 1.0 copy.11
  (3 shorter events, 0.0 us)
Async XLA Ops:
  10.8 55.3 %collective-permute-start.1 = (bf16[512,7168]{1,0:T(8,128)(2,1)}, bf16[512,7168]{1,0:T(8,128)(2,1)S(1)}, u32[]{:S(2)}, u32[]{:S(2)}) collective-permute-start(bf16[512,7168]{1,0:T(8,128)(2,1)} %own_h.1), channel_id=1, source_target_pairs={{0,4},{4,0},{1,5},{5,1},{2,6},{6,2},{3,7},{7,3},{8,12},{12,8},{9,1... | collective-permute-start | bytes 22020104 | tf_op jit(solution)/shard_map/ppermute | solution.py:285
  12.7 53.4 %collective-permute-start = (bf16[144,512]{1,0:T(8,128)(2,1)}, bf16[144,512]{1,0:T(8,128)(2,1)S(1)}, u32[]{:S(2)}, u32[]{:S(2)}) collective-permute-start(bf16[144,512]{1,0:T(8,128)(2,1)} %bitcast.15), channel_id=1, source_target_pairs={{0,4},{4,0},{1,5},{5,1},{2,6},{6,2},{3,7},{7,3},{8,12},{12,8},{9,1... | collective-permute-start | bytes 442376 | tf_op jit(solution)/shard_map/ppermute | solution.py:286
  66.0 9.8 %copy-start = (f32[1,28,144]{2,0,1:T(1,128)S(1)}, f32[1,28,144]{2,0,1:T(1,128)}, u32[]{:S(2)}) copy-start(f32[1,28,144]{2,0,1:T(1,128)} %param.11) | copy-start | bytes 48388
  72.4 17.5 %all-to-all-start.1 = ((bf16[4,144,896]{2,1,0:T(8,128)(2,1)}), bf16[4,144,896]{2,1,0:T(8,128)(2,1)S(1)}, u32[]{:S(2)}, u32[]{:S(2)}) async-start(bf16[4,144,896]{2,1,0:T(8,128)(2,1)} %grad_parts.1), calls=%async_computation.1 | async-start | bytes 2064384 | tf_op jit(solution)/shard_map/all_to_all | solution.py:271
  75.9 10.2 %collective-permute-start.2 = (f32[28,1,144]{2,1,0:T(1,128)S(1)}, f32[28,1,144]{2,1,0:T(1,128)S(1)}, u32[]{:S(2)}, u32[]{:S(2)}) collective-permute-start(f32[28,1,144]{2,1,0:T(1,128)S(1)} %bitcast.12), channel_id=1, source_target_pairs={{0,128},{128,0},{1,129},{129,1},{2,130},{130,2},{3,131},{131,3},{4... | collective-permute-start | bytes 48392 | tf_op jit(solution)/shard_map/ppermute | solution.py:291

commit v7 on v6

--- a/solution.py
+++ b/solution.py
@@ -48,36 +48,41 @@
     return acc
 
 
-def grad_body(place_at, x_at, info, seen, own_c, oth_c, own_h, oth_h, out, w_own, w_oth, edge):
-    step = pl.program_id(0)
-
-    @pl.when(step == 0)
-    def _():
-        lane = lane_iota(seen.shape[0])
-        rewards = jnp.where((lane < 8 * INFO) & (lane % INFO < 4), seen[...], 0).astype(f32)
-        labels = roll(seen[...], -4)
-        pos = lax.broadcasted_iota(jnp.int32, (1, LANE), 1)
-        for s in range(8):
-            core = place_at[0] % 2 if s < 4 else 1 - place_at[0] % 2
-            base = (x_at[0] * 2 + core) * INFO + s % 4
-            reward, label, length = info[base], info[base + 4], info[base + 8]
-            mates = jnp.where(labels == label, rewards, 0.0)
-            total = jnp.sum(mates, axis=(0, 1), keepdims=True)
-            square = jnp.sum(mates * mates, axis=(0, 1), keepdims=True)
-            mean = total / GROUP
-            var = square / GROUP - mean * mean
-            adv = (jnp.full((1, 1), reward, jnp.int32).astype(f32) - mean) / jnp.sqrt(var + 1.0)
-            live = jnp.where(pos < length, 1.0, 0.0)
-            scale = adv * live / jnp.full((1, 1), length, jnp.int32).astype(f32)
-            src, dst = (own_c, w_own) if s < 4 else (oth_c, w_oth)
-            at = (s % 4) * LANE
-            dst[:, at : at + LANE] = (src[:, at : at + LANE].astype(f32) * scale).astype(bf16)
-
-    block = jnp.dot(w_own[...], own_h[...], preferred_element_type=f32)
-    at = pl.multiple_of((2 * step + place_at[0] % 2) * ROWS, LANE)
-    block += jnp.dot(w_oth[...], oth_h[:, pl.ds(at, ROWS)], preferred_element_type=f32)
-
-    def place(j):
+def grad_body(place_at, x_at, info, seen, own_c, oth_c, own_h, oth_h, out, cot, wide, w_own, w_oth, edge, sems):
+    def column(j):
+        return pl.ds(pl.multiple_of((2 * j + place_at[0] % 2) * ROWS, LANE), ROWS)
+
+    copies = [pltpu.make_async_copy(own_c, cot, sems.at[4])]
+    copies += [pltpu.make_async_copy(own_h.at[:, column(j)], wide.at[j], sems.at[j]) for j in range(4)]
+    for copy in copies:
+        copy.start()
+
+    lane = lane_iota(seen.shape[0])
+    rewards = jnp.where((lane < 8 * INFO) & (lane % INFO < 4), seen[...], 0).astype(f32)
+    labels = roll(seen[...], -4)
+    row = lax.broadcasted_iota(jnp.int32, (8, LANE), 0)
+    pos = lax.broadcasted_iota(jnp.int32, (8, LANE), 1)
+    totals, squares = jnp.zeros((8, LANE), f32), jnp.zeros((8, LANE), f32)
+    reward, length = jnp.zeros((8, LANE), jnp.int32), jnp.ones((8, LANE), jnp.int32)
+    for s in range(8):
+        core = place_at[0] % 2 if s < 4 else 1 - place_at[0] % 2
+        base = (x_at[0] * 2 + core) * INFO + s % 4
+        mates = jnp.where(labels == info[base + 4], rewards, 0.0)
+        totals = jnp.where(row == s, jnp.sum(mates, axis=0, keepdims=True), totals)
+        squares = jnp.where(row == s, jnp.sum(mates * mates, axis=0, keepdims=True), squares)
+        reward = jnp.where(row == s, info[base], reward)
+        length = jnp.where(row == s, info[base + 8], length)
+    mean = jnp.sum(totals, axis=1, keepdims=True) / GROUP
+    var = jnp.sum(squares, axis=1, keepdims=True) / GROUP - mean * mean
+    adv = (reward.astype(f32) - mean) / jnp.sqrt(var + 1.0)
+    scale = adv * jnp.where(pos < length, 1.0, 0.0) / length.astype(f32)
+    copies[0].wait()
+    for s in range(8):
+        src, dst = (cot, w_own) if s < 4 else (oth_c, w_oth)
+        at = (s % 4) * LANE
+        dst[:, at : at + LANE] = (src[:, at : at + LANE].astype(f32) * scale[s : s + 1]).astype(bf16)
+
+    def place(j, block):
         lo, hi = j * PART, (j + 1) * PART
         tiles = lambda k: block[:, k * LANE : (k + 1) * LANE]
         for x in range(4):
@@ -91,36 +96,29 @@
                     edge[x] = acc
 
     for j in range(4):
-        pl.when(step == j)(lambda j=j: place(j))
+        other = jnp.dot(w_oth[...], oth_h[:, column(j)], preferred_element_type=f32)
+        copies[1 + j].wait()
+        place(j, jnp.dot(w_own[...], wide[j], preferred_element_type=f32) + other)
 
 
 def grad_parts(place_at, x_at, info, seen, own_c, oth_c, own_h, oth_h):
     tokens = own_h.shape[0]
-    half = pl.BlockSpec((tokens, ROWS), lambda j, place, x, info: (0, 2 * j + place[0] % 2))
-    whole = lambda shape: pl.BlockSpec(shape, lambda j, place, x, info: (0,) * len(shape))
+    scalars = pl.BlockSpec(memory_space=pltpu.SMEM)
+    in_place = pl.BlockSpec(memory_space=pl.ANY)
     return pl.pallas_call(
         grad_body,
         out_shape=pltpu.VMEM((4, COLS, ROWS), bf16),
-        grid_spec=pltpu.PrefetchScalarGridSpec(
-            num_scalar_prefetch=3,
-            grid=(4,),
-            in_specs=[
-                IN_VMEM,
-                whole(own_c.shape),
-                IN_VMEM,
-                half,
-                IN_VMEM,
-            ],
-            out_specs=whole((4, COLS, ROWS)),
-            scratch_shapes=[
-                pltpu.VMEM((COLS, tokens), bf16),
-                pltpu.VMEM((COLS, tokens), bf16),
-                pltpu.VMEM((4, COLS, LANE), f32),
-            ],
-        ),
-        compiler_params=pltpu.CompilerParams(
-            dimension_semantics=("arbitrary",), vmem_limit_bytes=24 << 20
-        ),
+        in_specs=[scalars, scalars, scalars, IN_VMEM, in_place, IN_VMEM, in_place, IN_VMEM],
+        out_specs=IN_VMEM,
+        scratch_shapes=[
+            pltpu.VMEM((COLS, tokens), bf16),
+            pltpu.VMEM((4, tokens, ROWS), bf16),
+            pltpu.VMEM((COLS, tokens), bf16),
+            pltpu.VMEM((COLS, tokens), bf16),
+            pltpu.VMEM((4, COLS, LANE), f32),
+            pltpu.SemaphoreType.DMA((5,)),
+        ],
+        compiler_params=pltpu.CompilerParams(vmem_limit_bytes=24 << 20),
         name="grad_parts",
     )(place_at, x_at, info, in_vmem(seen), in_hbm(own_c), in_vmem(oth_c), in_hbm(own_h), in_vmem(oth_h))
 

time: 160 us -> 158 us (0.988)
  no operation moved by 1% of the time
where the time goes in v7:
time: 158 us
  blocking collectives  127 us (80%)
  waiting for transfers between devices  11.6 us (7%)
  starting transfers between devices  10.2 us (6%)
  Pallas kernels  6.29 us (4%)
  local copies, waits for them, and re-layouts  1.58 us (1%)
    all_to_all x4, blocking collectives, exchange(): return lax.all_to_all(array, axis, split_axis=0, concat_axis=0, tiled=True)  103 us
    all_gather x1, blocking collectives, shards(): rollout = lax.all_gather(block.T[None], TP, axis=2, tiled=True)  14 us
    psum x1, blocking collectives, shards(): info = lax.psum(info, (X, CORE))  9.22 us
    ppermute x1, waiting for transfers between devices, shards(): other_master = lax.ppermute(later_master, ZA, swap)  7.81 us
    pallas_call x1, Pallas kernels, grad_parts(): pl.pallas_call(grad_body, out_shape=pltpu.VMEM((4, COLS, ROWS), bf16), in...  4.77 us
    all_to_all x1, waiting for transfers between devices, exchange(): return lax.all_to_all(array, axis, split_axis=0, concat_axis=0, tiled=True)  3.77 us
    all_to_all x1, starting transfers between devices, exchange(): return lax.all_to_all(array, axis, split_axis=0, concat_axis=0, tiled=True)  3.53 us
  transfers between devices with their start and end apart: 4, of which 2 were waited for; matrix products, arithmetic and copies ran while one was open for 0% of the time, Pallas kernels for 0%

profile of v7, /device:TPU:8, one launch (start us, length us, event | category | flops | bytes accessed | tf_op | source)
XLA Modules:
  0.0 157.9 jit_solution(11342031603428409618)
XLA Ops:
  0.7 0.9 add_dynamic-update-slice_fusion
  1.5 9.2 %psum.7.info = s32[128]{0:T(128)S(1)} all-reduce(s32[128]{0:T(128)S(1)} %add_dynamic-update-slice_fusion), channel_id=1, replica_groups=mesh['x'=4,'z_half'=2,'z_quad'=4,'z_hi'=4,'core'=2,'tp'=4] {'x','core'}, use_global_device_ids=true, to_apply=%region_0.1 | all-reduce | flops 128 | bytes 1024 | tf_op jit(solution)/shard_map/psum | solution.py:280
  10.8 1.9 %collective-permute-start.1 = (bf16[512,7168]{1,0:T(8,128)(2,1)}, bf16[512,7168]{1,0:T(8,128)(2,1)S(1)}, u32[]{:S(2)}, u32[]{:S(2)}) collective-permute-start(bf16[512,7168]{1,0:T(8,128)(2,1)} %own_h.1), channel_id=1, source_target_pairs={{0,4},{4,0},{1,5},{5,1},{2,6},{6,2},{3,7},{7,3},{8,12},{12,8},{9,1... | collective-permute-start | bytes 22020104 | tf_op jit(solution)/shard_map/ppermute | solution.py:283
  12.7 2.4 %collective-permute-start = (bf16[144,512]{1,0:T(8,128)(2,1)}, bf16[144,512]{1,0:T(8,128)(2,1)S(1)}, u32[]{:S(2)}, u32[]{:S(2)}) collective-permute-start(bf16[144,512]{1,0:T(8,128)(2,1)} %bitcast.15), channel_id=1, source_target_pairs={{0,4},{4,0},{1,5},{5,1},{2,6},{6,2},{3,7},{7,3},{8,12},{12,8},{9,1... | collective-permute-start | bytes 442376 | tf_op jit(solution)/shard_map/ppermute | solution.py:284
  15.1 50.9 %all_to_all.31 = s32[32,1,128]{2,1,0:T(1,128)S(1)} all-to-all(s32[32,1,128]{2,1,0:T(1,128)S(1)} %bitcast.17), channel_id=1, replica_groups=mesh['x'=4,'z_half'=2,'z_quad'=4,'z_hi'=4,'core'=2,'tp'=4] {'z_hi','z_ha..., dimensions={0} | all-to-all | bytes 32768 | tf_op jit(solution)/shard_map/all_to_all | solution.py:269
  66.0 0.0 collective-permute-done.oth_c
  66.0 0.0 collective-permute-done.1.oth_h
  66.0 0.0 copy-start
  66.0 4.8 %grad_parts.1 = bf16[4,144,896]{2,1,0:T(8,128)(2,1)} custom-call(s32[1]{0:T(128)} %bitcast.place_at, s32[1]{0:T(128)} %bitcast.1.x_at, s32[128]{0:T(128)S(1)} %psum.7.info, s32[32,128]{1,0:T(8,128)S(1)} %bitcast.11, bf16[144,512]{1,0:T(8,128)(2,1)} %bitcast.16, bf16[144,512]{1,0:T(8,128)(2,1)S(1)} %collective-permute-done.oth_c, bf16[512,7168]{1,0:T(8,128)(2,1)} %own_h.1, ...), custom_call_target="tpu_custom_call" | custom-call | tf_op jit(solution)/shard_map/grad_parts/pallas_call | solution.py:108
  70.8 3.5 %all-to-all-start.1 = ((bf16[4,144,896]{2,1,0:T(8,128)(2,1)}), bf16[4,144,896]{2,1,0:T(8,128)(2,1)S(1)}, u32[]{:S(2)}, u32[]{:S(2)}) async-start(bf16[4,144,896]{2,1,0:T(8,128)(2,1)} %grad_parts.1), calls=%async_computation.1 | async-start | bytes 2064384 | tf_op jit(solution)/shard_map/all_to_all | solution.py:269
  74.4 0.0 copy-done
  74.4 2.3 %collective-permute-start.2 = (f32[28,1,144]{2,1,0:T(1,128)S(1)}, f32[28,1,144]{2,1,0:T(1,128)S(1)}, u32[]{:S(2)}, u32[]{:S(2)}) collective-permute-start(f32[28,1,144]{2,1,0:T(1,128)S(1)} %bitcast.12), channel_id=1, source_target_pairs={{0,128},{128,0},{1,129},{129,1},{2,130},{130,2},{3,131},{131,3},{4... | collective-permute-start | bytes 48392 | tf_op jit(solution)/shard_map/ppermute | solution.py:289
  76.7 7.8 %collective-permute-done.2.other = f32[28,1,144]{2,1,0:T(1,128)S(1)} collective-permute-done((f32[28,1,144]{2,1,0:T(1,128)S(1)}, f32[28,1,144]{2,1,0:T(1,128)S(1)}, u32[]{:S(2)}, u32[]{:S(2)}) %collective-permute-start.2) | collective-permute-done | bytes 16160 | tf_op jit(solution)/shard_map/ppermute | solution.py:289
  84.5 3.8 %all-to-all-done.1.parts = bf16[4,144,896]{2,1,0:T(8,128)(2,1)S(1)} async-done(((bf16[4,144,896]{2,1,0:T(8,128)(2,1)}), bf16[4,144,896]{2,1,0:T(8,128)(2,1)S(1)}, u32[]{:S(2)}, u32[]{:S(2)}) %all-to-all-start.1) | async-done | bytes 1032224 | tf_op jit(solution)/shard_map/all_to_all | solution.py:269
  88.3 0.6 x_sum.1
  88.9 9.5 %all_to_all.32.parts = bf16[32,32,128]{2,1,0:T(8,128)(2,1)S(1)} all-to-all(bf16[32,32,128]{2,1,0:T(8,128)(2,1)S(1)} %x_sum.1), channel_id=1, replica_groups=mesh['x'=4,'z_half'=2,'z_quad'=4,'z_hi'=4,'core'=2,'tp'=4] {'z_quad'}, dimensions={0} | all-to-all | bytes 524288 | tf_op jit(solution)/shard_map/all_to_all | solution.py:269
  98.4 30.0 %all_to_all.33.parts = bf16[16,32,128]{2,1,0:T(8,128)(2,1)S(1)} all-to-all(bf16[16,32,128]{2,1,0:T(8,128)(2,1)S(1)} %quad_sum.1), channel_id=1, replica_groups=mesh['x'=4,'z_half'=2,'z_quad'=4,'z_hi'=4,'core'=2,'tp'=4] {'z_hi','z_ha..., dimensions={0} | all-to-all | bytes 262144 | tf_op jit(solution)/shard_map/all_to_all | solution.py:269
  128.4 0.3 z_sum.1
  128.8 12.9 %all_to_all.34.parts = bf16[32,32,128]{2,1,0:T(8,128)(2,1)S(1)} all-to-all(bf16[32,32,128]{2,1,0:T(8,128)(2,1)S(1)} %get-tuple-element.24), channel_id=1, replica_groups=mesh['x'=4,'z_half'=2,'z_quad'=4,'z_hi'=4,'core'=2,'tp'=4] {'x','z_quad'}, dimensions={0} | all-to-all | bytes 524288 | tf_op jit(solution)/shard_map/all_to_all | solution.py:269
  141.7 0.5 row_block.1
  142.3 0.6 copy.10
  142.9 14.0 %all-gather = bf16[896,576]{0,1:T(8,128)(2,1)S(1)} all-gather(bf16[896,144]{0,1:T(8,128)(2,1)S(1)} %bitcast.10), channel_id=2, replica_groups=mesh['x'=4,'z_half'=2,'z_quad'=4,'z_hi'=4,'core'=2,'tp'=4] {'tp'}, dimensions={1}, use_global_device_ids=true | all-gather | bytes 1290240 | tf_op jit(solution)/shard_map/all_gather | solution.py:295
  156.9 1.0 copy.11
  (3 shorter events, 0.0 us)
Async XLA Ops:
  10.8 55.3 %collective-permute-start.1 = (bf16[512,7168]{1,0:T(8,128)(2,1)}, bf16[512,7168]{1,0:T(8,128)(2,1)S(1)}, u32[]{:S(2)}, u32[]{:S(2)}) collective-permute-start(bf16[512,7168]{1,0:T(8,128)(2,1)} %own_h.1), channel_id=1, source_target_pairs={{0,4},{4,0},{1,5},{5,1},{2,6},{6,2},{3,7},{7,3},{8,12},{12,8},{9,1... | collective-permute-start | bytes 22020104 | tf_op jit(solution)/shard_map/ppermute | solution.py:283
  12.7 53.4 %collective-permute-start = (bf16[144,512]{1,0:T(8,128)(2,1)}, bf16[144,512]{1,0:T(8,128)(2,1)S(1)}, u32[]{:S(2)}, u32[]{:S(2)}) collective-permute-start(bf16[144,512]{1,0:T(8,128)(2,1)} %bitcast.15), channel_id=1, source_target_pairs={{0,4},{4,0},{1,5},{5,1},{2,6},{6,2},{3,7},{7,3},{8,12},{12,8},{9,1... | collective-permute-start | bytes 442376 | tf_op jit(solution)/shard_map/ppermute | solution.py:284
  66.0 8.3 %copy-start = (f32[1,28,144]{2,0,1:T(1,128)S(1)}, f32[1,28,144]{2,0,1:T(1,128)}, u32[]{:S(2)}) copy-start(f32[1,28,144]{2,0,1:T(1,128)} %param.11) | copy-start | bytes 48388
  70.8 17.5 %all-to-all-start.1 = ((bf16[4,144,896]{2,1,0:T(8,128)(2,1)}), bf16[4,144,896]{2,1,0:T(8,128)(2,1)S(1)}, u32[]{:S(2)}, u32[]{:S(2)}) async-start(bf16[4,144,896]{2,1,0:T(8,128)(2,1)} %grad_parts.1), calls=%async_computation.1 | async-start | bytes 2064384 | tf_op jit(solution)/shard_map/all_to_all | solution.py:269
  74.4 10.2 %collective-permute-start.2 = (f32[28,1,144]{2,1,0:T(1,128)S(1)}, f32[28,1,144]{2,1,0:T(1,128)S(1)}, u32[]{:S(2)}, u32[]{:S(2)}) collective-permute-start(f32[28,1,144]{2,1,0:T(1,128)S(1)} %bitcast.12), channel_id=1, source_target_pairs={{0,128},{128,0},{1,129},{129,1},{2,130},{130,2},{3,131},{131,3},{4... | collective-permute-start | bytes 48392 | tf_op jit(solution)/shard_map/ppermute | solution.py:289

commit v8 on v7

--- a/solution.py
+++ b/solution.py
@@ -48,7 +48,7 @@
     return acc
 
 
-def grad_body(place_at, x_at, info, seen, own_c, oth_c, own_h, oth_h, out, cot, wide, w_own, w_oth, edge, sems):
+def grad_body(place_at, x_at, info, seen, own_c, oth_c, own_h, oth_h, out, cot, wide, w_own, w_oth, edge, ready, sems, out_sems):
     def column(j):
         return pl.ds(pl.multiple_of((2 * j + place_at[0] % 2) * ROWS, LANE), ROWS)
 
@@ -91,7 +91,7 @@
                 acc = edge[x] if t * LANE < lo else jnp.zeros((COLS, LANE), f32)
                 acc = put(acc, tiles, x * PART + begin - lo, begin - t * LANE, end - begin)
                 if end == (t + 1) * LANE:
-                    out[x, :, t * LANE : end] = acc.astype(bf16)
+                    ready[x, :, t * LANE : end] = acc.astype(bf16)
                 else:
                     edge[x] = acc
 
@@ -99,6 +99,12 @@
         other = jnp.dot(w_oth[...], oth_h[:, column(j)], preferred_element_type=f32)
         copies[1 + j].wait()
         place(j, jnp.dot(w_own[...], wide[j], preferred_element_type=f32) + other)
+        tiles = slice(j * PART // LANE * LANE, (j + 1) * PART // LANE * LANE)
+        copy = pltpu.make_async_copy(ready.at[:, :, tiles], out.at[:, :, tiles], out_sems.at[j])
+        copy.start()
+        copies.append(copy)
+    for copy in copies[5:]:
+        copy.wait()
 
 
 def grad_parts(place_at, x_at, info, seen, own_c, oth_c, own_h, oth_h):
@@ -107,16 +113,18 @@
     in_place = pl.BlockSpec(memory_space=pl.ANY)
     return pl.pallas_call(
         grad_body,
-        out_shape=pltpu.VMEM((4, COLS, ROWS), bf16),
+        out_shape=jax.ShapeDtypeStruct((4, COLS, ROWS), bf16),
         in_specs=[scalars, scalars, scalars, IN_VMEM, in_place, IN_VMEM, in_place, IN_VMEM],
-        out_specs=IN_VMEM,
+        out_specs=in_place,
         scratch_shapes=[
             pltpu.VMEM((COLS, tokens), bf16),
             pltpu.VMEM((4, tokens, ROWS), bf16),
             pltpu.VMEM((COLS, tokens), bf16),
             pltpu.VMEM((COLS, tokens), bf16),
             pltpu.VMEM((4, COLS, LANE), f32),
+            pltpu.VMEM((4, COLS, ROWS), bf16),
             pltpu.SemaphoreType.DMA((5,)),
+            pltpu.SemaphoreType.DMA((4,)),
         ],
         compiler_params=pltpu.CompilerParams(vmem_limit_bytes=24 << 20),
         name="grad_parts",
@@ -224,7 +232,9 @@
     )(place_at, in_vmem(parts), in_vmem(mine), in_vmem(other))
 
 
-def rows_body(parts, out, wide, rest):
+def rows_body(parts, grad, out, grad_out, wide, rest, sem):
+    copy = pltpu.make_async_copy(grad, grad_out, sem)
+    copy.start()
     for d in range(32):
         x, half, quad = d // 8, d % 8 // 4, d % 4
         piece = parts[(x * 4 + quad) * 2 + half].astype(f32)
@@ -241,20 +251,22 @@
                     acc = put(acc, lambda k: wide[d], q * OWN + lo - d * OWN, lo - t * LANE, hi - lo)
             out[q * STRIPE : (q + 1) * STRIPE, at] = acc.astype(bf16)
         out[4 * STRIPE :, at] = rest[at, :].T[:REST].astype(bf16)
-
-
-def row_block(parts):
+    copy.wait()
+
+
+def row_block(parts, grad):
     return pl.pallas_call(
         rows_body,
-        out_shape=pltpu.VMEM((COLS, ROWS), bf16),
-        in_specs=[IN_VMEM],
-        out_specs=IN_VMEM,
+        out_shape=(pltpu.VMEM((COLS, ROWS), bf16), jax.ShapeDtypeStruct(grad.shape, f32)),
+        in_specs=[IN_VMEM, IN_VMEM],
+        out_specs=(IN_VMEM, pl.BlockSpec(memory_space=pl.ANY)),
         scratch_shapes=[
             pltpu.VMEM((32, STRIPE, LANE), f32),
             pltpu.VMEM((ROWS, LANE), f32),
+            pltpu.SemaphoreType.DMA,
         ],
         name="row_block",
-    )(in_vmem(parts))
+    )(in_vmem(parts), in_vmem(grad))
 
 
 def in_vmem(array):
@@ -290,10 +302,9 @@
     parts, later_master, other_master = lax.optimization_barrier((parts, later_master, other_master))
     parts = quad_sum(exchange(x_sum(parts), ZB))
     grad, copies = z_sum(place_at[None], exchange(parts, (ZH, ZA)), later_master, other_master)
-    block = row_block(exchange(copies, (X, ZB)))
-    block, grad = lax.optimization_barrier((block, grad))
-    rollout = lax.all_gather(block.T[None], TP, axis=2, tiled=True)
-    return (grad.transpose(1, 0, 2), rollout)
+    block, grad = row_block(exchange(copies, (X, ZB)), grad)
+    rollout = lax.all_gather(block, TP, axis=0, tiled=True)
+    return (grad.transpose(1, 0, 2), rollout.T[None])
 
 
 def solution(mesh):

time: 158 us -> 158 us (level)
  no operation moved by 1% of the time
where the time goes in v8:
time: 158 us
  blocking collectives  127 us (80%)
  waiting for transfers between devices  11.6 us (7%)
  starting transfers between devices  10.2 us (6%)
  Pallas kernels  6.61 us (4%)
    all_to_all x4, blocking collectives, exchange(): return lax.all_to_all(array, axis, split_axis=0, concat_axis=0, tiled=True)  103 us
    all_gather x1, blocking collectives, shards(): rollout = lax.all_gather(block, TP, axis=0, tiled=True)  14 us
    psum x1, blocking collectives, shards(): info = lax.psum(info, (X, CORE))  9.22 us
    ppermute x1, waiting for transfers between devices, shards(): other_master = lax.ppermute(later_master, ZA, swap)  7.81 us
    pallas_call x1, Pallas kernels, grad_parts(): pl.pallas_call(grad_body, out_shape=jax.ShapeDtypeStruct((4, COLS, ROWS),...  4.55 us
    all_to_all x1, waiting for transfers between devices, exchange(): return lax.all_to_all(array, axis, split_axis=0, concat_axis=0, tiled=True)  3.77 us
    all_to_all x1, starting transfers between devices, exchange(): return lax.all_to_all(array, axis, split_axis=0, concat_axis=0, tiled=True)  3.53 us
  transfers between devices with their start and end apart: 4, of which 2 were waited for; matrix products, arithmetic and copies ran while one was open for 0% of the time, Pallas kernels for 0%

profile of v8, /device:TPU:8, one launch (start us, length us, event | category | flops | bytes accessed | tf_op | source)
XLA Modules:
  0.0 157.6 jit_solution(6345650234582727530)
XLA Ops:
  0.7 0.9 add_dynamic-update-slice_fusion
  1.5 9.2 %psum.7.info = s32[128]{0:T(128)S(1)} all-reduce(s32[128]{0:T(128)S(1)} %add_dynamic-update-slice_fusion), channel_id=1, replica_groups=mesh['x'=4,'z_half'=2,'z_quad'=4,'z_hi'=4,'core'=2,'tp'=4] {'x','core'}, use_global_device_ids=true, to_apply=%region_0.1 | all-reduce | flops 128 | bytes 1024 | tf_op jit(solution)/shard_map/psum | solution.py:292
  10.8 1.9 %collective-permute-start.1 = (bf16[512,7168]{1,0:T(8,128)(2,1)}, bf16[512,7168]{1,0:T(8,128)(2,1)S(1)}, u32[]{:S(2)}, u32[]{:S(2)}) collective-permute-start(bf16[512,7168]{1,0:T(8,128)(2,1)} %own_h.1), channel_id=1, source_target_pairs={{0,4},{4,0},{1,5},{5,1},{2,6},{6,2},{3,7},{7,3},{8,12},{12,8},{9,1... | collective-permute-start | bytes 22020104 | tf_op jit(solution)/shard_map/ppermute | solution.py:295
  12.7 2.4 %collective-permute-start = (bf16[144,512]{1,0:T(8,128)(2,1)}, bf16[144,512]{1,0:T(8,128)(2,1)S(1)}, u32[]{:S(2)}, u32[]{:S(2)}) collective-permute-start(bf16[144,512]{1,0:T(8,128)(2,1)} %bitcast.14), channel_id=1, source_target_pairs={{0,4},{4,0},{1,5},{5,1},{2,6},{6,2},{3,7},{7,3},{8,12},{12,8},{9,1... | collective-permute-start | bytes 442376 | tf_op jit(solution)/shard_map/ppermute | solution.py:296
  15.1 50.9 %all_to_all.31 = s32[32,1,128]{2,1,0:T(1,128)S(1)} all-to-all(s32[32,1,128]{2,1,0:T(1,128)S(1)} %bitcast.16), channel_id=1, replica_groups=mesh['x'=4,'z_half'=2,'z_quad'=4,'z_hi'=4,'core'=2,'tp'=4] {'z_hi','z_ha..., dimensions={0} | all-to-all | bytes 32768 | tf_op jit(solution)/shard_map/all_to_all | solution.py:281
  66.0 0.0 collective-permute-done.oth_c
  66.0 0.0 collective-permute-done.1.oth_h
  66.0 0.0 copy-start
  66.0 4.6 %grad_parts.1 = bf16[4,144,896]{2,1,0:T(8,128)(2,1)} custom-call(s32[1]{0:T(128)} %bitcast.place_at, s32[1]{0:T(128)} %bitcast.1.x_at, s32[128]{0:T(128)S(1)} %psum.7.info, s32[32,128]{1,0:T(8,128)S(1)} %bitcast.10, bf16[144,512]{1,0:T(8,128)(2,1)} %bitcast.15, bf16[144,512]{1,0:T(8,128)(2,1)S(1)} %collective-permute-done.oth_c, bf16[512,7168]{1,0:T(8,128)(2,1)} %own_h.1, ...), custom_call_target="tpu_custom_call" | custom-call | tf_op jit(solution)/shard_map/grad_parts/pallas_call | solution.py:114
  70.6 3.5 %all-to-all-start.1 = ((bf16[4,144,896]{2,1,0:T(8,128)(2,1)}), bf16[4,144,896]{2,1,0:T(8,128)(2,1)S(1)}, u32[]{:S(2)}, u32[]{:S(2)}) async-start(bf16[4,144,896]{2,1,0:T(8,128)(2,1)} %grad_parts.1), calls=%async_computation.1 | async-start | bytes 2064384 | tf_op jit(solution)/shard_map/all_to_all | solution.py:281
  74.1 0.0 copy-done
  74.1 2.3 %collective-permute-start.2 = (f32[28,1,144]{2,1,0:T(1,128)S(1)}, f32[28,1,144]{2,1,0:T(1,128)S(1)}, u32[]{:S(2)}, u32[]{:S(2)}) collective-permute-start(f32[28,1,144]{2,1,0:T(1,128)S(1)} %bitcast.11), channel_id=1, source_target_pairs={{0,128},{128,0},{1,129},{129,1},{2,130},{130,2},{3,131},{131,3},{4... | collective-permute-start | bytes 48392 | tf_op jit(solution)/shard_map/ppermute | solution.py:301
  76.5 7.8 %collective-permute-done.2.other = f32[28,1,144]{2,1,0:T(1,128)S(1)} collective-permute-done((f32[28,1,144]{2,1,0:T(1,128)S(1)}, f32[28,1,144]{2,1,0:T(1,128)S(1)}, u32[]{:S(2)}, u32[]{:S(2)}) %collective-permute-start.2) | collective-permute-done | bytes 16160 | tf_op jit(solution)/shard_map/ppermute | solution.py:301
  84.3 3.8 %all-to-all-done.1.parts = bf16[4,144,896]{2,1,0:T(8,128)(2,1)S(1)} async-done(((bf16[4,144,896]{2,1,0:T(8,128)(2,1)}), bf16[4,144,896]{2,1,0:T(8,128)(2,1)S(1)}, u32[]{:S(2)}, u32[]{:S(2)}) %all-to-all-start.1) | async-done | bytes 1032224 | tf_op jit(solution)/shard_map/all_to_all | solution.py:281
  88.1 0.6 x_sum.1
  88.7 9.5 %all_to_all.32.parts = bf16[32,32,128]{2,1,0:T(8,128)(2,1)S(1)} all-to-all(bf16[32,32,128]{2,1,0:T(8,128)(2,1)S(1)} %x_sum.1), channel_id=1, replica_groups=mesh['x'=4,'z_half'=2,'z_quad'=4,'z_hi'=4,'core'=2,'tp'=4] {'z_quad'}, dimensions={0} | all-to-all | bytes 524288 | tf_op jit(solution)/shard_map/all_to_all | solution.py:281
  98.2 30.0 %all_to_all.33.parts = bf16[16,32,128]{2,1,0:T(8,128)(2,1)S(1)} all-to-all(bf16[16,32,128]{2,1,0:T(8,128)(2,1)S(1)} %quad_sum.1), channel_id=1, replica_groups=mesh['x'=4,'z_half'=2,'z_quad'=4,'z_hi'=4,'core'=2,'tp'=4] {'z_hi','z_ha..., dimensions={0} | all-to-all | bytes 262144 | tf_op jit(solution)/shard_map/all_to_all | solution.py:281
  128.2 0.3 z_sum.1
  128.6 12.9 %all_to_all.34.parts = bf16[32,32,128]{2,1,0:T(8,128)(2,1)S(1)} all-to-all(bf16[32,32,128]{2,1,0:T(8,128)(2,1)S(1)} %get-tuple-element.24), channel_id=1, replica_groups=mesh['x'=4,'z_half'=2,'z_quad'=4,'z_hi'=4,'core'=2,'tp'=4] {'x','z_quad'}, dimensions={0} | all-to-all | bytes 524288 | tf_op jit(solution)/shard_map/all_to_all | solution.py:281
  141.5 1.1 row_block.1
  142.6 14.0 %all_gather.3 = bf16[576,896]{1,0:T(8,128)(2,1)S(1)} all-gather(bf16[144,896]{1,0:T(8,128)(2,1)S(1)} %get-tuple-element.27), channel_id=1, replica_groups=mesh['x'=4,'z_half'=2,'z_quad'=4,'z_hi'=4,'core'=2,'tp'=4] {'tp'}, dimensions={0}, use_global_device_ids=true | all-gather | bytes 1290240 | tf_op jit(solution)/shard_map/all_gather | solution.py:306
  156.6 1.0 copy.10
  (3 shorter events, 0.0 us)
Async XLA Ops:
  10.8 55.3 %collective-permute-start.1 = (bf16[512,7168]{1,0:T(8,128)(2,1)}, bf16[512,7168]{1,0:T(8,128)(2,1)S(1)}, u32[]{:S(2)}, u32[]{:S(2)}) collective-permute-start(bf16[512,7168]{1,0:T(8,128)(2,1)} %own_h.1), channel_id=1, source_target_pairs={{0,4},{4,0},{1,5},{5,1},{2,6},{6,2},{3,7},{7,3},{8,12},{12,8},{9,1... | collective-permute-start | bytes 22020104 | tf_op jit(solution)/shard_map/ppermute | solution.py:295
  12.7 53.4 %collective-permute-start = (bf16[144,512]{1,0:T(8,128)(2,1)}, bf16[144,512]{1,0:T(8,128)(2,1)S(1)}, u32[]{:S(2)}, u32[]{:S(2)}) collective-permute-start(bf16[144,512]{1,0:T(8,128)(2,1)} %bitcast.14), channel_id=1, source_target_pairs={{0,4},{4,0},{1,5},{5,1},{2,6},{6,2},{3,7},{7,3},{8,12},{12,8},{9,1... | collective-permute-start | bytes 442376 | tf_op jit(solution)/shard_map/ppermute | solution.py:296
  66.0 8.1 %copy-start = (f32[1,28,144]{2,0,1:T(1,128)S(1)}, f32[1,28,144]{2,0,1:T(1,128)}, u32[]{:S(2)}) copy-start(f32[1,28,144]{2,0,1:T(1,128)} %param.11) | copy-start | bytes 48388
  70.6 17.5 %all-to-all-start.1 = ((bf16[4,144,896]{2,1,0:T(8,128)(2,1)}), bf16[4,144,896]{2,1,0:T(8,128)(2,1)S(1)}, u32[]{:S(2)}, u32[]{:S(2)}) async-start(bf16[4,144,896]{2,1,0:T(8,128)(2,1)} %grad_parts.1), calls=%async_computation.1 | async-start | bytes 2064384 | tf_op jit(solution)/shard_map/all_to_all | solution.py:281
  74.1 10.2 %collective-permute-start.2 = (f32[28,1,144]{2,1,0:T(1,128)S(1)}, f32[28,1,144]{2,1,0:T(1,128)S(1)}, u32[]{:S(2)}, u32[]{:S(2)}) collective-permute-start(f32[28,1,144]{2,1,0:T(1,128)S(1)} %bitcast.11), channel_id=1, source_target_pairs={{0,128},{128,0},{1,129},{129,1},{2,130},{130,2},{3,131},{131,3},{4... | collective-permute-start | bytes 48392 | tf_op jit(solution)/shard_map/ppermute | solution.py:301

commit v9 on v8

--- a/solution.py
+++ b/solution.py
@@ -173,7 +173,7 @@
         )
         j, half = divmod(p, 2)
         for to in range(2):
-            out[j * 4 + to * 2 + half] = total.astype(bf16)
+            out[to * 8 + j * 2 + half] = total.astype(bf16)
 
 
 def quad_sum(parts):
@@ -294,14 +294,14 @@
     copies, later_hidden, later_cot, info = lax.optimization_barrier((copies, hidden, cot, info))
     other_hidden = lax.ppermute(later_hidden, CORE, swap)
     other_cot = lax.ppermute(later_cot, CORE, swap)
-    seen = exchange(copies, (ZH, ZA, ZB))
+    seen = exchange(copies, (ZB, ZA, ZH))
     parts = grad_parts(place_at[None], x[None], info, seen, cot, other_cot, hidden, other_hidden)
     parts, later_master = lax.optimization_barrier((parts, master.transpose(1, 0, 2)))
     parts = exchange(parts, X)
     other_master = lax.ppermute(later_master, ZA, swap)
     parts, later_master, other_master = lax.optimization_barrier((parts, later_master, other_master))
     parts = quad_sum(exchange(x_sum(parts), ZB))
-    grad, copies = z_sum(place_at[None], exchange(parts, (ZH, ZA)), later_master, other_master)
+    grad, copies = z_sum(place_at[None], exchange(parts, (ZA, ZH)), later_master, other_master)
     block, grad = row_block(exchange(copies, (X, ZB)), grad)
     rollout = lax.all_gather(block, TP, axis=0, tiled=True)
     return (grad.transpose(1, 0, 2), rollout.T[None])

time: 158 us -> 157 us (level)
  blocking collectives: 127 us -> 125 us
where the time goes in v9:
time: 157 us; the launch traced here: 156 us
  blocking collectives  125 us (80%)
  waiting for transfers between devices  10.9 us (7%)
  starting transfers between devices  10.8 us (7%)
  Pallas kernels  6.6 us (4%)
    all_to_all x4, blocking collectives, exchange(): return lax.all_to_all(array, axis, split_axis=0, concat_axis=0, tiled=True)  102 us
    all_gather x1, blocking collectives, shards(): rollout = lax.all_gather(block, TP, axis=0, tiled=True)  14 us
    psum x1, blocking collectives, shards(): info = lax.psum(info, (X, CORE))  9.22 us
    ppermute x1, waiting for transfers between devices, shards(): other_master = lax.ppermute(later_master, ZA, swap)  7.61 us
    pallas_call x1, Pallas kernels, grad_parts(): pl.pallas_call(grad_body, out_shape=jax.ShapeDtypeStruct((4, COLS, ROWS),...  4.54 us
    all_to_all x1, starting transfers between devices, exchange(): return lax.all_to_all(array, axis, split_axis=0, concat_axis=0, tiled=True)  3.53 us
    all_to_all x1, waiting for transfers between devices, exchange(): return lax.all_to_all(array, axis, split_axis=0, concat_axis=0, tiled=True)  3.31 us
  transfers between devices with their start and end apart: 4, of which 2 were waited for; matrix products, arithmetic and copies ran while one was open for 0% of the time, Pallas kernels for 0%

profile of v9, /device:TPU:8, one launch (start us, length us, event | category | flops | bytes accessed | tf_op | source)
XLA Modules:
  0.0 156.2 jit_solution(638810214645346964)
XLA Ops:
  0.7 0.9 add_dynamic-update-slice_fusion
  1.5 9.2 %psum.7.info = s32[128]{0:T(128)S(1)} all-reduce(s32[128]{0:T(128)S(1)} %add_dynamic-update-slice_fusion), channel_id=1, replica_groups=mesh['x'=4,'z_half'=2,'z_quad'=4,'z_hi'=4,'core'=2,'tp'=4] {'x','core'}, use_global_device_ids=true, to_apply=%region_0.1 | all-reduce | flops 128 | bytes 1024 | tf_op jit(solution)/shard_map/psum | solution.py:292
  10.8 1.9 %collective-permute-start.1 = (bf16[512,7168]{1,0:T(8,128)(2,1)}, bf16[512,7168]{1,0:T(8,128)(2,1)S(1)}, u32[]{:S(2)}, u32[]{:S(2)}) collective-permute-start(bf16[512,7168]{1,0:T(8,128)(2,1)} %own_h.1), channel_id=1, source_target_pairs={{0,4},{4,0},{1,5},{5,1},{2,6},{6,2},{3,7},{7,3},{8,12},{12,8},{9,1... | collective-permute-start | bytes 22020104 | tf_op jit(solution)/shard_map/ppermute | solution.py:295
  12.7 2.4 %collective-permute-start = (bf16[144,512]{1,0:T(8,128)(2,1)}, bf16[144,512]{1,0:T(8,128)(2,1)S(1)}, u32[]{:S(2)}, u32[]{:S(2)}) collective-permute-start(bf16[144,512]{1,0:T(8,128)(2,1)} %bitcast.14), channel_id=1, source_target_pairs={{0,4},{4,0},{1,5},{5,1},{2,6},{6,2},{3,7},{7,3},{8,12},{12,8},{9,1... | collective-permute-start | bytes 442376 | tf_op jit(solution)/shard_map/ppermute | solution.py:296
  15.1 50.3 %all_to_all.31 = s32[32,1,128]{2,1,0:T(1,128)S(1)} all-to-all(s32[32,1,128]{2,1,0:T(1,128)S(1)} %bitcast.16), channel_id=1, replica_groups=mesh['x'=4,'z_half'=2,'z_quad'=4,'z_hi'=4,'core'=2,'tp'=4] {'z_quad','z_..., dimensions={0} | all-to-all | bytes 32768 | tf_op jit(solution)/shard_map/all_to_all | solution.py:281
  65.4 0.0 collective-permute-done.oth_c
  65.4 0.0 collective-permute-done.1.oth_h
  65.4 0.0 copy-start
  65.4 4.5 %grad_parts.1 = bf16[4,144,896]{2,1,0:T(8,128)(2,1)} custom-call(s32[1]{0:T(128)} %bitcast.place_at, s32[1]{0:T(128)} %bitcast.1.x_at, s32[128]{0:T(128)S(1)} %psum.7.info, s32[32,128]{1,0:T(8,128)S(1)} %bitcast.10, bf16[144,512]{1,0:T(8,128)(2,1)} %bitcast.15, bf16[144,512]{1,0:T(8,128)(2,1)S(1)} %collective-permute-done.oth_c, bf16[512,7168]{1,0:T(8,128)(2,1)} %own_h.1, ...), custom_call_target="tpu_custom_call" | custom-call | tf_op jit(solution)/shard_map/grad_parts/pallas_call | solution.py:114
  70.0 3.5 %all-to-all-start.1 = ((bf16[4,144,896]{2,1,0:T(8,128)(2,1)}), bf16[4,144,896]{2,1,0:T(8,128)(2,1)S(1)}, u32[]{:S(2)}, u32[]{:S(2)}) async-start(bf16[4,144,896]{2,1,0:T(8,128)(2,1)} %grad_parts.1), calls=%async_computation.1 | async-start | bytes 2064384 | tf_op jit(solution)/shard_map/all_to_all | solution.py:281
  73.5 0.0 copy-done
  73.5 3.0 %collective-permute-start.2 = (f32[28,1,144]{2,1,0:T(1,128)S(1)}, f32[28,1,144]{2,1,0:T(1,128)S(1)}, u32[]{:S(2)}, u32[]{:S(2)}) collective-permute-start(f32[28,1,144]{2,1,0:T(1,128)S(1)} %bitcast.11), channel_id=1, source_target_pairs={{0,128},{128,0},{1,129},{129,1},{2,130},{130,2},{3,131},{131,3},{4... | collective-permute-start | bytes 48392 | tf_op jit(solution)/shard_map/ppermute | solution.py:301
  76.5 7.6 %collective-permute-done.2.other = f32[28,1,144]{2,1,0:T(1,128)S(1)} collective-permute-done((f32[28,1,144]{2,1,0:T(1,128)S(1)}, f32[28,1,144]{2,1,0:T(1,128)S(1)}, u32[]{:S(2)}, u32[]{:S(2)}) %collective-permute-start.2) | collective-permute-done | bytes 16160 | tf_op jit(solution)/shard_map/ppermute | solution.py:301
  84.1 3.3 %all-to-all-done.1.parts = bf16[4,144,896]{2,1,0:T(8,128)(2,1)S(1)} async-done(((bf16[4,144,896]{2,1,0:T(8,128)(2,1)}), bf16[4,144,896]{2,1,0:T(8,128)(2,1)S(1)}, u32[]{:S(2)}, u32[]{:S(2)}) %all-to-all-start.1) | async-done | bytes 1032224 | tf_op jit(solution)/shard_map/all_to_all | solution.py:281
  87.4 0.6 x_sum.1
  88.0 9.5 %all_to_all.32.parts = bf16[32,32,128]{2,1,0:T(8,128)(2,1)S(1)} all-to-all(bf16[32,32,128]{2,1,0:T(8,128)(2,1)S(1)} %x_sum.1), channel_id=1, replica_groups=mesh['x'=4,'z_half'=2,'z_quad'=4,'z_hi'=4,'core'=2,'tp'=4] {'z_quad'}, dimensions={0} | all-to-all | bytes 524288 | tf_op jit(solution)/shard_map/all_to_all | solution.py:281
  97.6 26.9 %all_to_all.33.parts = bf16[16,32,128]{2,1,0:T(8,128)(2,1)S(1)} all-to-all(bf16[16,32,128]{2,1,0:T(8,128)(2,1)S(1)} %quad_sum.1), channel_id=1, replica_groups=mesh['x'=4,'z_half'=2,'z_quad'=4,'z_hi'=4,'core'=2,'tp'=4] {'z_half','z_..., dimensions={0} | all-to-all | bytes 262144 | tf_op jit(solution)/shard_map/all_to_all | solution.py:281
  124.5 0.3 z_sum.1
  124.8 15.3 %all_to_all.34.parts = bf16[32,32,128]{2,1,0:T(8,128)(2,1)S(1)} all-to-all(bf16[32,32,128]{2,1,0:T(8,128)(2,1)S(1)} %get-tuple-element.24), channel_id=1, replica_groups=mesh['x'=4,'z_half'=2,'z_quad'=4,'z_hi'=4,'core'=2,'tp'=4] {'x','z_quad'}, dimensions={0} | all-to-all | bytes 524288 | tf_op jit(solution)/shard_map/all_to_all | solution.py:281
  140.1 1.1 row_block.1
  141.2 14.0 %all_gather.3 = bf16[576,896]{1,0:T(8,128)(2,1)S(1)} all-gather(bf16[144,896]{1,0:T(8,128)(2,1)S(1)} %get-tuple-element.27), channel_id=1, replica_groups=mesh['x'=4,'z_half'=2,'z_quad'=4,'z_hi'=4,'core'=2,'tp'=4] {'tp'}, dimensions={0}, use_global_device_ids=true | all-gather | bytes 1290240 | tf_op jit(solution)/shard_map/all_gather | solution.py:306
  155.2 1.0 copy.10
  (3 shorter events, 0.0 us)
Async XLA Ops:
  10.8 54.7 %collective-permute-start.1 = (bf16[512,7168]{1,0:T(8,128)(2,1)}, bf16[512,7168]{1,0:T(8,128)(2,1)S(1)}, u32[]{:S(2)}, u32[]{:S(2)}) collective-permute-start(bf16[512,7168]{1,0:T(8,128)(2,1)} %own_h.1), channel_id=1, source_target_pairs={{0,4},{4,0},{1,5},{5,1},{2,6},{6,2},{3,7},{7,3},{8,12},{12,8},{9,1... | collective-permute-start | bytes 22020104 | tf_op jit(solution)/shard_map/ppermute | solution.py:295
  12.7 52.8 %collective-permute-start = (bf16[144,512]{1,0:T(8,128)(2,1)}, bf16[144,512]{1,0:T(8,128)(2,1)S(1)}, u32[]{:S(2)}, u32[]{:S(2)}) collective-permute-start(bf16[144,512]{1,0:T(8,128)(2,1)} %bitcast.14), channel_id=1, source_target_pairs={{0,4},{4,0},{1,5},{5,1},{2,6},{6,2},{3,7},{7,3},{8,12},{12,8},{9,1... | collective-permute-start | bytes 442376 | tf_op jit(solution)/shard_map/ppermute | solution.py:296
  65.4 8.1 %copy-start = (f32[1,28,144]{2,0,1:T(1,128)S(1)}, f32[1,28,144]{2,0,1:T(1,128)}, u32[]{:S(2)}) copy-start(f32[1,28,144]{2,0,1:T(1,128)} %param.11) | copy-start | bytes 48388
  70.0 17.4 %all-to-all-start.1 = ((bf16[4,144,896]{2,1,0:T(8,128)(2,1)}), bf16[4,144,896]{2,1,0:T(8,128)(2,1)S(1)}, u32[]{:S(2)}, u32[]{:S(2)}) async-start(bf16[4,144,896]{2,1,0:T(8,128)(2,1)} %grad_parts.1), calls=%async_computation.1 | async-start | bytes 2064384 | tf_op jit(solution)/shard_map/all_to_all | solution.py:281
  73.5 10.6 %collective-permute-start.2 = (f32[28,1,144]{2,1,0:T(1,128)S(1)}, f32[28,1,144]{2,1,0:T(1,128)S(1)}, u32[]{:S(2)}, u32[]{:S(2)}) collective-permute-start(f32[28,1,144]{2,1,0:T(1,128)S(1)} %bitcast.11), channel_id=1, source_target_pairs={{0,128},{128,0},{1,129},{129,1},{2,130},{130,2},{3,131},{131,3},{4... | collective-permute-start | bytes 48392 | tf_op jit(solution)/shard_map/ppermute | solution.py:301
